TPU v7x, 32 devices: a 4x4x1 block of a 4x4x8 slice. The times are simulated.
32 devices in a mesh: parts: 1 (over z), data: 32 (over y, x, core).
Axes of the slice: x: 4, y: 4, z: 1, core: 2. Of those that a mesh axis runs over, the one named last changes fastest.
The devices are a block of a 4x4x8 slice.
Arguments:
- feats: bfloat16 [32768, 784], P('data')
- labels: int32 [32768], P('data')
- w_in: float32 [784, 2, 400], P(None, 'parts')
- w_out: float32 [2, 400], P('parts')
- mom_in: float32 [784, 2, 400], P(None, 'parts')
- mom_out: float32 [2, 400], P('parts')
Outputs:
- output 1: float32 [784, 2, 400], P(None, 'parts')
- output 2: float32 [2, 400], P('parts')
- output 3: float32 [784, 2, 400], P(None, 'parts')
- output 4: float32 [2, 400], P('parts')
- output 5: float32 [2], P('parts')
All inputs are finite; a program needn't handle non-finite values.
Results may differ from a plain program's by a relative error of at most 0.001.
Values are sent between devices in bfloat16 or wider.
A program may use at most 768 MiB of HBM per device.

v0:
```python
import math
import jax
import jax.numpy as jnp
from jax import lax
from jax.sharding import PartitionSpec as P

LEAPS = 16
PRIOR_VAR = 1.0


def local_terms(x_rows, lab_rows, w_flat, pos_out):
    num_chain, hidden = pos_out.shape
    num_rows = x_rows.shape[0]
    pre_act = jnp.dot(x_rows, w_flat, preferred_element_type=jnp.float32).reshape(num_rows, num_chain, hidden)
    hidden_act = jnp.tanh(pre_act)
    logits = jnp.sum(hidden_act * pos_out, axis=-1)
    residual = lab_rows[:, None] - jax.nn.sigmoid(logits)
    grad_out = jnp.sum(hidden_act * residual[:, :, None], axis=0)
    back_grad = (residual[:, :, None] * pos_out * (1.0 - hidden_act * hidden_act)).astype(jnp.bfloat16)
    grad_in = lax.dot_general(x_rows, back_grad.reshape(num_rows, num_chain * hidden), (((0,), (0,)), ((), ())), preferred_element_type=jnp.float32)
    return grad_in.reshape(w_flat.shape[0], num_chain, hidden), grad_out, logits


def solution(mesh):
    row_spec = P('data', None)
    label_spec = P('data')
    in_spec = P(None, 'parts', None)
    out_spec = P('parts', None)
    chain_spec = P('parts')

    def run_chains(feats, labels, w_in, w_out, mom_in, mom_out):
        num_rows, num_feat = feats.shape
        hidden = w_in.shape[2]
        step_size = 1.0 / math.sqrt(num_rows * (num_feat + hidden))
        half_step = 0.5 * step_size

        def device_body(x_rows, y_rows, pos_in, pos_out, vel_in, vel_out):
            lab_rows = y_rows.astype(jnp.float32)
            num_chain = pos_out.shape[0]

            def log_post_grad(pos_in, pos_out):
                w_flat = pos_in.astype(jnp.bfloat16).reshape(num_feat, num_chain * hidden)
                grad_in, grad_out, logits = local_terms(x_rows, lab_rows, w_flat, pos_out)
                grad_in, grad_out = lax.psum((grad_in, grad_out), 'data')
                return grad_in - pos_in / PRIOR_VAR, grad_out - pos_out / PRIOR_VAR, logits

            def leap_step(step_index, state_now):
                pos_in, pos_out, vel_in, vel_out = state_now
                pos_in = pos_in + step_size * vel_in
                pos_out = pos_out + step_size * vel_out
                grad_in, grad_out, logits = log_post_grad(pos_in, pos_out)
                return pos_in, pos_out, vel_in + step_size * grad_in, vel_out + step_size * grad_out

            grad_in, grad_out, logits = log_post_grad(pos_in, pos_out)
            vel_in = vel_in + half_step * grad_in
            vel_out = vel_out + half_step * grad_out
            pos_in, pos_out, vel_in, vel_out = lax.fori_loop(0, LEAPS - 1, leap_step, (pos_in, pos_out, vel_in, vel_out))
            pos_in = pos_in + step_size * vel_in
            pos_out = pos_out + step_size * vel_out
            grad_in, grad_out, logits = log_post_grad(pos_in, pos_out)
            vel_in = vel_in + half_step * grad_in
            vel_out = vel_out + half_step * grad_out
            row_loss = jnp.sum(jax.nn.softplus(logits) - lab_rows[:, None] * logits, axis=0)
            row_loss = lax.psum(row_loss, 'data')
            energy = row_loss + (jnp.sum(pos_in * pos_in, axis=(0, 2)) + jnp.sum(pos_out * pos_out, axis=1)) / (2.0 * PRIOR_VAR) + 0.5 * (jnp.sum(vel_in * vel_in, axis=(0, 2)) + jnp.sum(vel_out * vel_out, axis=1))
            return pos_in, pos_out, vel_in, vel_out, energy

        mapped = jax.shard_map(device_body, mesh=mesh, in_specs=(row_spec, label_spec, in_spec, out_spec, in_spec, out_spec), out_specs=(in_spec, out_spec, in_spec, out_spec, chain_spec), check_vma=False)
        return mapped(feats, labels, w_in, w_out, mom_in, mom_out)

    return run_chains
```

profile of v0, /device:TPU:97, one launch (start us, length us, event | category | flops | bytes accessed | tf_op | source)
XLA Modules:
  0.0 2073.3 jit_solution(524742811450162200)
XLA Ops:
  20.8 50.3 %psum.50 = f32[2,400]{1,0:T(2,128)S(1)} all-reduce(f32[2,400]{1,0:T(2,128)S(1)} %get-tuple-element.82), channel_id=1, replica_groups=mesh['parts'=1,'data'=32] {'data'}, use_global_device_ids=true, to_apply=%region_3.0 | all-reduce | flops 800 | bytes 6400 | tf_op jit(solution)/shard_map/psum | solution.py:44
  71.1 52.6 %all-reduce.5.cloned.1.call-done = f32[784,2,400]{0,2,1:T(8,128)} async-done(((f32[784,2,400]{0,2,1:T(8,128)}), f32[784,2,400]{0,2,1:T(8,128)}) %all-reduce.5.cloned.1.call-update) | async-done | bytes 2508816 | tf_op jit(solution)/shard_map/psum | solution.py:44
  128.4 1819.7 %while.16 = (s32[]{:T(128)}, f32[784,2,400]{0,2,1:T(8,128)S(1)}, f32[2,400]{1,0:T(2,128)S(1)}, f32[784,2,400]{0,2,1:T(8,128)}, f32[2,400]{1,0:T(2,128)S(1)}, /*i...) while((s32[]{:T(128)}, f32[784,2,400]{0,2,1:T(8,128)S(1)}, f32[2,400]{1,0:T(2,128)S(1)}, ...), condition=%wide.region_9.0_spmd, body=%wide.region_4.0_spmd.sunk | while | flops 2580784384 | bytes 109203696 | solution.py:57
  147.8 46.5 %psum.57 = f32[2,400]{1,0:T(2,128)S(1)} all-reduce(f32[2,400]{1,0:T(2,128)S(1)} %reduce_sum.129), channel_id=1, replica_groups=mesh['parts'=1,'data'=32] {'data'}, use_global_device_ids=true, to_apply=%region_8.0 | all-reduce | flops 800 | bytes 6400 | tf_op jit(solution)/shard_map/while/body/eval_jaxpr/psum | solution.py:44
  194.3 49.7 %all-reduce.9.cloned.1.call-done = f32[784,2,400]{0,2,1:T(8,128)} async-done(((f32[784,2,400]{0,2,1:T(8,128)}), f32[784,2,400]{0,2,1:T(8,128)}) %all-reduce.9.cloned.1.call-update) | async-done | bytes 2508816 | tf_op jit(solution)/shard_map/while/body/eval_jaxpr/psum | solution.py:44
  315.6 49.7 %all-reduce.9.cloned.1.call-done = f32[784,2,400]{0,2,1:T(8,128)} async-done(((f32[784,2,400]{0,2,1:T(8,128)}), f32[784,2,400]{0,2,1:T(8,128)}) %all-reduce.9.cloned.1.call-update) | async-done | bytes 2508816 | tf_op jit(solution)/shard_map/while/body/eval_jaxpr/psum | solution.py:44
  390.5 46.5 %psum.57 = f32[2,400]{1,0:T(2,128)S(1)} all-reduce(f32[2,400]{1,0:T(2,128)S(1)} %reduce_sum.129), channel_id=1, replica_groups=mesh['parts'=1,'data'=32] {'data'}, use_global_device_ids=true, to_apply=%region_8.0 | all-reduce | flops 800 | bytes 6400 | tf_op jit(solution)/shard_map/while/body/eval_jaxpr/psum | solution.py:44
  436.9 49.7 %all-reduce.9.cloned.1.call-done = f32[784,2,400]{0,2,1:T(8,128)} async-done(((f32[784,2,400]{0,2,1:T(8,128)}), f32[784,2,400]{0,2,1:T(8,128)}) %all-reduce.9.cloned.1.call-update) | async-done | bytes 2508816 | tf_op jit(solution)/shard_map/while/body/eval_jaxpr/psum | solution.py:44
  558.3 49.7 %all-reduce.9.cloned.1.call-done = f32[784,2,400]{0,2,1:T(8,128)} async-done(((f32[784,2,400]{0,2,1:T(8,128)}), f32[784,2,400]{0,2,1:T(8,128)}) %all-reduce.9.cloned.1.call-update) | async-done | bytes 2508816 | tf_op jit(solution)/shard_map/while/body/eval_jaxpr/psum | solution.py:44
  679.6 49.7 %all-reduce.9.cloned.1.call-done = f32[784,2,400]{0,2,1:T(8,128)} async-done(((f32[784,2,400]{0,2,1:T(8,128)}), f32[784,2,400]{0,2,1:T(8,128)}) %all-reduce.9.cloned.1.call-update) | async-done | bytes 2508816 | tf_op jit(solution)/shard_map/while/body/eval_jaxpr/psum | solution.py:44
  800.9 49.7 %all-reduce.9.cloned.1.call-done = f32[784,2,400]{0,2,1:T(8,128)} async-done(((f32[784,2,400]{0,2,1:T(8,128)}), f32[784,2,400]{0,2,1:T(8,128)}) %all-reduce.9.cloned.1.call-update) | async-done | bytes 2508816 | tf_op jit(solution)/shard_map/while/body/eval_jaxpr/psum | solution.py:44
  922.2 49.7 %all-reduce.9.cloned.1.call-done = f32[784,2,400]{0,2,1:T(8,128)} async-done(((f32[784,2,400]{0,2,1:T(8,128)}), f32[784,2,400]{0,2,1:T(8,128)}) %all-reduce.9.cloned.1.call-update) | async-done | bytes 2508816 | tf_op jit(solution)/shard_map/while/body/eval_jaxpr/psum | solution.py:44
  997.0 46.5 %psum.57 = f32[2,400]{1,0:T(2,128)S(1)} all-reduce(f32[2,400]{1,0:T(2,128)S(1)} %reduce_sum.129), channel_id=1, replica_groups=mesh['parts'=1,'data'=32] {'data'}, use_global_device_ids=true, to_apply=%region_8.0 | all-reduce | flops 800 | bytes 6400 | tf_op jit(solution)/shard_map/while/body/eval_jaxpr/psum | solution.py:44
  1043.5 49.7 %all-reduce.9.cloned.1.call-done = f32[784,2,400]{0,2,1:T(8,128)} async-done(((f32[784,2,400]{0,2,1:T(8,128)}), f32[784,2,400]{0,2,1:T(8,128)}) %all-reduce.9.cloned.1.call-update) | async-done | bytes 2508816 | tf_op jit(solution)/shard_map/while/body/eval_jaxpr/psum | solution.py:44
  1118.4 46.5 %psum.57 = f32[2,400]{1,0:T(2,128)S(1)} all-reduce(f32[2,400]{1,0:T(2,128)S(1)} %reduce_sum.129), channel_id=1, replica_groups=mesh['parts'=1,'data'=32] {'data'}, use_global_device_ids=true, to_apply=%region_8.0 | all-reduce | flops 800 | bytes 6400 | tf_op jit(solution)/shard_map/while/body/eval_jaxpr/psum | solution.py:44
  1164.8 49.7 %all-reduce.9.cloned.1.call-done = f32[784,2,400]{0,2,1:T(8,128)} async-done(((f32[784,2,400]{0,2,1:T(8,128)}), f32[784,2,400]{0,2,1:T(8,128)}) %all-reduce.9.cloned.1.call-update) | async-done | bytes 2508816 | tf_op jit(solution)/shard_map/while/body/eval_jaxpr/psum | solution.py:44
  1286.2 49.7 %all-reduce.9.cloned.1.call-done = f32[784,2,400]{0,2,1:T(8,128)} async-done(((f32[784,2,400]{0,2,1:T(8,128)}), f32[784,2,400]{0,2,1:T(8,128)}) %all-reduce.9.cloned.1.call-update) | async-done | bytes 2508816 | tf_op jit(solution)/shard_map/while/body/eval_jaxpr/psum | solution.py:44
  1407.5 49.7 %all-reduce.9.cloned.1.call-done = f32[784,2,400]{0,2,1:T(8,128)} async-done(((f32[784,2,400]{0,2,1:T(8,128)}), f32[784,2,400]{0,2,1:T(8,128)}) %all-reduce.9.cloned.1.call-update) | async-done | bytes 2508816 | tf_op jit(solution)/shard_map/while/body/eval_jaxpr/psum | solution.py:44
  1528.8 49.7 %all-reduce.9.cloned.1.call-done = f32[784,2,400]{0,2,1:T(8,128)} async-done(((f32[784,2,400]{0,2,1:T(8,128)}), f32[784,2,400]{0,2,1:T(8,128)}) %all-reduce.9.cloned.1.call-update) | async-done | bytes 2508816 | tf_op jit(solution)/shard_map/while/body/eval_jaxpr/psum | solution.py:44
  1650.1 49.7 %all-reduce.9.cloned.1.call-done = f32[784,2,400]{0,2,1:T(8,128)} async-done(((f32[784,2,400]{0,2,1:T(8,128)}), f32[784,2,400]{0,2,1:T(8,128)}) %all-reduce.9.cloned.1.call-update) | async-done | bytes 2508816 | tf_op jit(solution)/shard_map/while/body/eval_jaxpr/psum | solution.py:44
  1724.9 46.5 %psum.57 = f32[2,400]{1,0:T(2,128)S(1)} all-reduce(f32[2,400]{1,0:T(2,128)S(1)} %reduce_sum.129), channel_id=1, replica_groups=mesh['parts'=1,'data'=32] {'data'}, use_global_device_ids=true, to_apply=%region_8.0 | all-reduce | flops 800 | bytes 6400 | tf_op jit(solution)/shard_map/while/body/eval_jaxpr/psum | solution.py:44
  1771.4 49.7 %all-reduce.9.cloned.1.call-done = f32[784,2,400]{0,2,1:T(8,128)} async-done(((f32[784,2,400]{0,2,1:T(8,128)}), f32[784,2,400]{0,2,1:T(8,128)}) %all-reduce.9.cloned.1.call-update) | async-done | bytes 2508816 | tf_op jit(solution)/shard_map/while/body/eval_jaxpr/psum | solution.py:44
  1892.7 49.7 %all-reduce.9.cloned.1.call-done = f32[784,2,400]{0,2,1:T(8,128)} async-done(((f32[784,2,400]{0,2,1:T(8,128)}), f32[784,2,400]{0,2,1:T(8,128)}) %all-reduce.9.cloned.1.call-update) | async-done | bytes 2508816 | tf_op jit(solution)/shard_map/while/body/eval_jaxpr/psum | solution.py:44
  2013.0 48.5 %all-reduce.7.cloned.1.call-done = f32[784,2,400]{0,2,1:T(8,128)} async-done(((f32[784,2,400]{0,2,1:T(8,128)}), f32[784,2,400]{0,2,1:T(8,128)}) %all-reduce.7.cloned.1.call-update) | async-done | bytes 2508816 | tf_op jit(solution)/shard_map/psum | solution.py:44
  (403 shorter events, 928.9 us)
Async XLA Ops:
  7.2 116.5 %all-reduce.5.cloned.1.call-start = ((), (), s32[]{:S(2)}) async-start(), calls=%async_computation | async-start | bytes 5734400 | tf_op jit(solution)/shard_map/psum | solution.py:44
  16.6 54.4 %copy-start.12 = (f32[2,400]{1,0:T(2,128)S(1)}, f32[2,400]{1,0:T(2,128)}, u32[]{:S(2)}) copy-start(f32[2,400]{1,0:T(2,128)} %param.13) | copy-start | bytes 9604
  128.4 115.7 %all-reduce.9.cloned.1.call-start = ((), (), s32[]{:S(2)}) async-start(), calls=%async_computation.2 | async-start | bytes 5734400 | tf_op jit(solution)/shard_map/while/body/eval_jaxpr/psum | solution.py:44
  244.1 5.7 copy-start.2
  249.7 115.6 %all-reduce.9.cloned.1.call-start = ((), (), s32[]{:S(2)}) async-start(), calls=%async_computation.2 | async-start | bytes 5734400 | tf_op jit(solution)/shard_map/while/body/eval_jaxpr/psum | solution.py:44
  365.4 5.7 copy-start.2
  371.0 115.7 %all-reduce.9.cloned.1.call-start = ((), (), s32[]{:S(2)}) async-start(), calls=%async_computation.2 | async-start | bytes 5734400 | tf_op jit(solution)/shard_map/while/body/eval_jaxpr/psum | solution.py:44
  486.7 5.7 copy-start.2
  492.3 115.6 %all-reduce.9.cloned.1.call-start = ((), (), s32[]{:S(2)}) async-start(), calls=%async_computation.2 | async-start | bytes 5734400 | tf_op jit(solution)/shard_map/while/body/eval_jaxpr/psum | solution.py:44
  613.7 115.6 %all-reduce.9.cloned.1.call-start = ((), (), s32[]{:S(2)}) async-start(), calls=%async_computation.2 | async-start | bytes 5734400 | tf_op jit(solution)/shard_map/while/body/eval_jaxpr/psum | solution.py:44
  729.3 5.7 copy-start.2
  735.0 115.7 %all-reduce.9.cloned.1.call-start = ((), (), s32[]{:S(2)}) async-start(), calls=%async_computation.2 | async-start | bytes 5734400 | tf_op jit(solution)/shard_map/while/body/eval_jaxpr/psum | solution.py:44
  856.3 115.6 %all-reduce.9.cloned.1.call-start = ((), (), s32[]{:S(2)}) async-start(), calls=%async_computation.2 | async-start | bytes 5734400 | tf_op jit(solution)/shard_map/while/body/eval_jaxpr/psum | solution.py:44
  977.6 115.6 %all-reduce.9.cloned.1.call-start = ((), (), s32[]{:S(2)}) async-start(), calls=%async_computation.2 | async-start | bytes 5734400 | tf_op jit(solution)/shard_map/while/body/eval_jaxpr/psum | solution.py:44
  1098.9 115.7 %all-reduce.9.cloned.1.call-start = ((), (), s32[]{:S(2)}) async-start(), calls=%async_computation.2 | async-start | bytes 5734400 | tf_op jit(solution)/shard_map/while/body/eval_jaxpr/psum | solution.py:44
  1220.2 115.6 %all-reduce.9.cloned.1.call-start = ((), (), s32[]{:S(2)}) async-start(), calls=%async_computation.2 | async-start | bytes 5734400 | tf_op jit(solution)/shard_map/while/body/eval_jaxpr/psum | solution.py:44
  1341.5 115.6 %all-reduce.9.cloned.1.call-start = ((), (), s32[]{:S(2)}) async-start(), calls=%async_computation.2 | async-start | bytes 5734400 | tf_op jit(solution)/shard_map/while/body/eval_jaxpr/psum | solution.py:44
  1462.8 115.7 %all-reduce.9.cloned.1.call-start = ((), (), s32[]{:S(2)}) async-start(), calls=%async_computation.2 | async-start | bytes 5734400 | tf_op jit(solution)/shard_map/while/body/eval_jaxpr/psum | solution.py:44
  1584.2 115.6 %all-reduce.9.cloned.1.call-start = ((), (), s32[]{:S(2)}) async-start(), calls=%async_computation.2 | async-start | bytes 5734400 | tf_op jit(solution)/shard_map/while/body/eval_jaxpr/psum | solution.py:44
  1705.5 115.6 %all-reduce.9.cloned.1.call-start = ((), (), s32[]{:S(2)}) async-start(), calls=%async_computation.2 | async-start | bytes 5734400 | tf_op jit(solution)/shard_map/while/body/eval_jaxpr/psum | solution.py:44
  1826.8 115.7 %all-reduce.9.cloned.1.call-start = ((), (), s32[]{:S(2)}) async-start(), calls=%async_computation.2 | async-start | bytes 5734400 | tf_op jit(solution)/shard_map/while/body/eval_jaxpr/psum | solution.py:44
  1948.1 113.3 %all-reduce.7.cloned.1.call-start = ((), (), s32[]{:S(2)}) async-start(), calls=%async_computation.1 | async-start | bytes 5734400 | tf_op jit(solution)/shard_map/psum | solution.py:44
  1948.2 64.0 %copy-start.10 = (f32[2,400]{1,0:T(2,128)}, f32[2,400]{1,0:T(2,128)S(1)}, u32[]{:S(2)}) copy-start(f32[2,400]{1,0:T(2,128)S(1)} %get-tuple-element.75) | copy-start | bytes 9604
  1962.8 98.6 %copy-start.3 = (f32[784,2,400]{0,2,1:T(8,128)S(1)}, f32[784,2,400]{0,2,1:T(8,128)}, u32[]{:S(2)}) copy-start(f32[784,2,400]{0,2,1:T(8,128)} %get-tuple-element.46) | copy-start | bytes 7526404
  (62 other events, 195.2 us)
Sparse Core Ops, SparseCore 0:
  20.9 102.7 all-reduce.4
  145.6 98.4 all-reduce.8
  266.9 98.4 all-reduce.8
  388.2 98.4 all-reduce.8
  509.5 98.4 all-reduce.8
  630.8 98.4 all-reduce.8
  752.1 98.4 all-reduce.8
  873.5 98.4 all-reduce.8
  994.8 98.4 all-reduce.8
  1116.1 98.4 all-reduce.8
  1237.4 98.4 all-reduce.8
  1358.7 98.4 all-reduce.8
  1480.0 98.4 all-reduce.8
  1601.4 98.4 all-reduce.8
  1722.7 98.4 all-reduce.8
  1844.0 98.4 all-reduce.8
  1962.9 98.4 all-reduce.6
where the time goes:
time: 2080 us; the launch traced here: 2070 us
  waiting for transfers between devices  848 us (41%)
  blocking collectives  793 us (38%)
  other arithmetic  191 us (9%)
  local copies, waits for them, and re-layouts  133 us (6%)
  matrix products  92.8 us (4%)
    psum x17, waiting for transfers between devices, log_post_grad(): grad_in, grad_out = lax.psum((grad_in, grad_out), 'data')  847 us
    psum x17, blocking collectives, log_post_grad(): grad_in, grad_out = lax.psum((grad_in, grad_out), 'data')  793 us
    add x15, other arithmetic, leap_step(): vel_in + step_size * grad_in  84.8 us
    dot_general x17, local copies, waits for them, and re-layouts, local_terms(): lax.dot_general(x_rows, back_grad.reshape(num_rows, num_chain * hidden),...  68.6 us
    dot_general x17, matrix products, local_terms(): lax.dot_general(x_rows, back_grad.reshape(num_rows, num_chain * hidden),...  61.1 us
    while x120, local copies, waits for them, and re-layouts  48.9 us
    convert_element_type x16, other arithmetic, log_post_grad(): w_flat = pos_in.astype(jnp.bfloat16).reshape(num_feat, num_chain * hidden)  48.6 us
  transfers between devices with their start and end apart: 17, of which 17 were waited for; matrix products, arithmetic and copies ran while one was open for 2% of the time, Pallas kernels for 0%

commit v1 on v0

v1 whole, which is shorter than its diff:
```python
import functools
import math

import jax
import jax.numpy as jnp
from jax import lax
from jax.experimental import pallas as pl
from jax.experimental.pallas import tpu as pltpu
from jax.sharding import PartitionSpec as P

LEAPS = 16
PRIOR_VAR = 1.0
LANE = 128
PACK = 16
MESH_ID = pl.DeviceIdType.MESH


def _kernel(cfg, xt_hbm, lab_ref, w_hbm, m_hbm, wo_ref, mo_ref, fin_w, fin_m, misc_ref,
            xt, x, ybuf, wload, wb, abuf, bbuf, gacc, g2acc, gsend, rsbuf, pos, mom, w2b, m2b, w2z, wag, zbuf, ztot,
            fin, obuf, lsem, isend, irecv, ysend, yrecv, zsend, zrecv, rsend, rrecv, asend, arecv, fsend, frecv, osem):
    side, hidden, feat, rows, hs, step = cfg
    half = side // 2
    nshard = 2 * side
    nfull = feat // LANE
    rem = feat - nfull * LANE
    nrow = hs // PACK
    nunit = nrow * nfull + 1
    own = -(-nunit // side)
    urows = own * PACK
    kpad = xt.shape[0]
    nlt = rows // LANE
    groups = zsend.shape[1]
    per_group = nshard // groups
    f32, bf16 = jnp.float32, jnp.bfloat16

    me = lax.axis_index('data')
    core = me % 2
    xx = (me // 2) % side
    yy = me // (2 * side)

    def fold(y, x_):
        return (x_ // half + y // half) % 2

    q = (core + fold(yy, xx)) % 2
    zpos = xx * (1 - q) + yy * q
    rpos = yy * (1 - q) + xx * q

    def device(z, r, role):
        x2 = z * (1 - role) + r * role
        y2 = r * (1 - role) + z * role
        return {'data': (y2 * side + x2) * 2 + (role + fold(y2, x2)) % 2}

    zpeer = [device((zpos + d) % side, rpos, q) for d in range(side)]
    rpeer = [device(zpos, (rpos + d) % side, q) for d in range(side)]
    partner = device(rpos, zpos, 1 - q)

    def remote(src, dst, ssem, rsem, dev):
        return pltpu.make_async_remote_copy(src_ref=src, dst_ref=dst, send_sem=ssem, recv_sem=rsem,
                                            device_id=dev, device_id_type=MESH_ID)

    start = jnp.minimum(zpos * hs, hidden - hs)
    start = pl.multiple_of(start, 8)
    cut = zpos * hs - start

    own_slot = 2 * zpos + q
    par_slot = 2 * zpos + (1 - q)

    def xcols(slot):
        return xt.at[pl.ds(0, feat), pl.ds(pl.multiple_of(slot * rows, rows), rows)]

    load_x = pltpu.make_async_copy(xt_hbm, xcols(own_slot), lsem.at[0])
    load_w = pltpu.make_async_copy(w_hbm.at[q, pl.ds(start, hs), :], wload.at[0], lsem.at[1])
    load_m = pltpu.make_async_copy(m_hbm.at[q, pl.ds(start, hs), :], wload.at[1], lsem.at[2])
    load_x.start()
    load_w.start()
    load_m.start()

    barrier = pltpu.get_barrier_semaphore()
    for dev in zpeer[1:] + rpeer[1:] + [partner]:
        pl.semaphore_signal(barrier, inc=1, device_id=dev, device_id_type=MESH_ID)
    pl.semaphore_wait(barrier, 2 * side - 1)

    def ship(i, slot, dslot, dev):
        cx = remote(xcols(slot), xcols(dslot), isend.at[i], irecv.at[i], dev)
        cy = remote(ybuf.at[slot], ybuf.at[dslot], ysend.at[i], yrecv.at[i], dev)
        cx.start()
        cy.start()
        return cx, cy

    def landed(pair):
        pair[0].wait_recv()
        pair[1].wait_recv()

    def turn(slot):
        def body(t, _):
            off = pl.multiple_of(slot * rows + t * LANE, LANE)
            x[pl.ds(off, LANE), :] = xt[:, pl.ds(off, LANE)].T
            return 0
        lax.fori_loop(0, rows // LANE, body, 0)

    ybuf[own_slot] = lab_ref[...]
    xt[pl.ds(feat, kpad - feat), :] = jnp.zeros((kpad - feat, nshard * rows), bf16)
    load_x.wait()
    up, down, far = (zpos + 1) % side, (zpos + side - 1) % side, (zpos + 2) % side
    s0 = ship(0, own_slot, 2 * rpos + q, partner)
    s1 = ship(1, own_slot, own_slot, zpeer[1])
    s4 = ship(4, own_slot, own_slot, zpeer[side - 1])
    turn(own_slot)

    lane = lax.broadcasted_iota(jnp.int32, (PACK, LANE), 1)
    lane8 = lax.broadcasted_iota(jnp.int32, (8, LANE), 1)
    sub8 = lax.broadcasted_iota(jnp.int32, (8, LANE), 0)

    def unit_at(u):
        return u // own, (u % own) * PACK

    def pack(src, dst, width):
        for i in range(nrow):
            for k in range(nfull):
                o, j = unit_at(i * nfull + k)
                dst[o, j:j + PACK, :] = src[i * PACK:(i + 1) * PACK, k * LANE:(k + 1) * LANE]
        o, j = unit_at(nunit - 1)
        acc = jnp.zeros((PACK, LANE), f32)
        for i in range(nrow):
            v = src[i * PACK:(i + 1) * PACK, nfull * LANE:nfull * LANE + width]
            if width < LANE:
                v = jnp.concatenate([v, jnp.zeros((PACK, LANE - width), f32)], axis=1)
            acc = acc + (pltpu.roll(v, i * rem, 1) if i else v)
        dst[o, j:j + PACK, :] = acc

    for o in range(side):
        for u in range(nunit, side * own):
            if u // own == o:
                gsend[o, (u % own) * PACK:(u % own + 1) * PACK, :] = jnp.zeros((PACK, LANE), f32)
    load_w.wait()
    load_m.wait()
    pack(wload.at[1], gsend, rem)
    mom[...] = gsend[rpos, 0:urows, :]
    pack(wload.at[0], gsend, rem)
    pos[...] = gsend[rpos, 0:urows, :]
    wb[:, nfull * LANE:] = jnp.zeros((hs, kpad - nfull * LANE), bf16)
    wb[:, 0:feat] = wload[0].astype(bf16)

    def column(ref, dst):
        width = -(-hidden // LANE) * LANE
        v = jnp.concatenate([ref[pl.ds(q, 1), :], jnp.zeros((1, width - hidden), f32)], axis=1)
        lanes = lax.broadcasted_iota(jnp.int32, (8, width), 1)
        subs = lax.broadcasted_iota(jnp.int32, (8, width), 0)
        v = jnp.broadcast_to(v, (8, width))
        for i in range(hs // 8):
            hit = jnp.where(lanes == start + i * 8 + subs, v, 0.0)
            dst[i * 8:(i + 1) * 8, :] = jnp.broadcast_to(jnp.sum(hit, axis=1, keepdims=True), (8, LANE))

    column(wo_ref, w2b)
    column(mo_ref, m2b)

    landed(s0)
    s2 = ship(2, par_slot, par_slot, zpeer[1])
    s5 = ship(5, par_slot, par_slot, zpeer[side - 1])
    turn(par_slot)
    landed(s1)
    s3 = ship(3, 2 * down + q, 2 * down + q, zpeer[1])
    turn(2 * down + q)
    landed(s4)
    turn(2 * up + q)
    landed(s5)
    s6 = ship(6, 2 * up + (1 - q), 2 * up + (1 - q), zpeer[side - 1])
    turn(2 * up + (1 - q))
    landed(s2)
    turn(2 * down + (1 - q))
    landed(s3)
    turn(2 * far + q)
    landed(s6)
    turn(2 * far + (1 - q))
    for pair in (s0, s1, s2, s3, s4, s5, s6):
        pair[0].wait_send()
        pair[1].wait_send()

    rowid = lax.broadcasted_iota(jnp.int32, (hs, LANE), 0)

    def z_copy(par, g, d):
        block = pl.ds(g * per_group, per_group)
        return remote(zbuf.at[par, zpos, block], zbuf.at[par, zpos, block],
                      zsend.at[par, g, d], zrecv.at[par, g, d], zpeer[d])

    def r_copy(d):
        return remote(gsend.at[(rpos + d) % side], rsbuf.at[rpos], rsend.at[d], rrecv.at[d], rpeer[d])

    def a_copy(d):
        return remote(wag.at[rpos], wag.at[rpos], asend.at[d], arecv.at[d], rpeer[d])

    def fin_ring(arr, d):
        return remote(fin.at[arr, q, zpos, rpos], fin.at[arr, q, zpos, rpos],
                      fsend.at[arr, d], frecv.at[arr, d], rpeer[d])

    def fin_cross(arr, d):
        return remote(fin.at[arr, q, zpos], fin.at[arr, q, zpos],
                      fsend.at[arr, side + d], frecv.at[arr, side + d], zpeer[d])

    def fin_pair(arr):
        return remote(fin.at[arr, q], fin.at[arr, q], fsend.at[arr, 0], frecv.at[arr, 0], partner)

    def gradient(k, _):
        par = k % 2
        w2z[...] = jnp.where(rowid >= cut, w2b[...], 0.0)

        def forward(g, _):
            for bb in range(per_group):
                b = g * per_group + bb
                off = pl.multiple_of(b * rows, rows)
                for n in range(rows // 256):
                    pre = jnp.dot(wb[...], xt[:, pl.ds(off + n * 256, 256)], preferred_element_type=f32)
                    act = jnp.tanh(pre)
                    abuf[b, :, n * 256:(n + 1) * 256] = act
                    for h in range(2):
                        part = jnp.sum(act[:, h * LANE:(h + 1) * LANE] * w2z[...], axis=0, keepdims=True)
                        zbuf[par, zpos, b, 2 * n + h:2 * n + h + 1, :] = part
            for d in range(1, side):
                z_copy(par, g, d).start()
            return 0

        lax.fori_loop(0, groups, forward, 0)
        gacc[...] = jnp.zeros_like(gacc)
        g2acc[...] = jnp.zeros_like(g2acc)

        def backward(g, _):
            for d in range(1, side):
                z_copy(par, g, d).wait_recv()
            for bb in range(per_group):
                b = g * per_group + bb
                off = pl.multiple_of(b * rows, rows)
                logit = zbuf[par, 0, b]
                for s in range(1, side):
                    logit = logit + zbuf[par, s, b]
                ztot[b] = logit
                res = ybuf[b].astype(f32) - jax.nn.sigmoid(logit)
                for n in range(nlt):
                    act = abuf[b, :, n * LANE:(n + 1) * LANE]
                    rr = jnp.broadcast_to(res[n:n + 1, :], (hs, LANE))
                    g2acc[...] += rr * act
                    bbuf[bb, :, n * LANE:(n + 1) * LANE] = ((rr * w2b[...]) * (1.0 - act * act)).astype(bf16)
                gacc[...] += jnp.dot(bbuf[bb], x[pl.ds(off, rows), :], preferred_element_type=f32)
            return 0

        lax.fori_loop(0, groups, backward, 0)
        pack(gacc, gsend, LANE)
        g2 = jnp.zeros((8, LANE), f32)
        for i in range(hs // 8):
            col = jnp.sum(g2acc[i * 8:(i + 1) * 8, :], axis=1, keepdims=True)
            g2 = jnp.where(lane8 == i, jnp.broadcast_to(col, (8, LANE)), g2)
        for o in range(side):
            gsend[o, urows:urows + 8, :] = g2
        for d in range(1, side):
            r_copy(d).start()
        rsbuf[rpos] = gsend[rpos]
        for g in range(groups):
            for d in range(1, side):
                z_copy(par, g, d).wait_send()
        for d in range(1, side):
            r_copy(d).wait_recv()
        total = rsbuf[0]
        for s in range(1, side):
            total = total + rsbuf[s]
        coef = jnp.where((k == 0) | (k == LEAPS), 0.5 * step, step).astype(f32)
        mom[...] = mom[...] + coef * (total[0:urows] - pos[...] / PRIOR_VAR)
        for i in range(hs // 8):
            blk = slice(i * 8, (i + 1) * 8)
            gcol = jnp.broadcast_to(total[urows:urows + 8, i:i + 1], (8, LANE))
            m2b[blk, :] = m2b[blk, :] + coef * (gcol - w2b[blk, :] / PRIOR_VAR)
        for d in range(1, side):
            r_copy(d).wait_send()

        @pl.when(k < LEAPS)
        def _():
            pos[...] = pos[...] + step * mom[...]
            w2b[...] = w2b[...] + step * m2b[...]
            wag[rpos] = pos[...].astype(bf16)
            for d in range(1, side):
                a_copy(d).start()
            for d in range(1, side):
                a_copy(d).wait_recv()
            for i in range(nrow):
                for kk in range(nfull):
                    o, j = unit_at(i * nfull + kk)
                    wb[i * PACK:(i + 1) * PACK, kk * LANE:(kk + 1) * LANE] = wag[o, j:j + PACK, :]
            o, j = unit_at(nunit - 1)
            left = wag[o, j:j + PACK, :].astype(f32)
            for i in range(nrow):
                v = pltpu.roll(left, LANE - i * rem, 1) if i else left
                wb[i * PACK:(i + 1) * PACK, nfull * LANE:] = jnp.where(lane < rem, v, 0.0).astype(bf16)
            for d in range(1, side):
                a_copy(d).wait_send()

        return 0

    lax.fori_loop(0, LEAPS + 1, gradient, 0)

    i0 = cut // PACK
    sq = jnp.zeros((PACK, LANE), f32)
    for j in range(own):
        u = own * rpos + j
        p_ = pos[j * PACK:(j + 1) * PACK, :]
        v_ = mom[j * PACK:(j + 1) * PACK, :]
        group_id = jnp.where(u == nunit - 1, lane // rem, u // nfull + 0 * lane)
        sq = sq + jnp.where(group_id >= i0, p_ * p_ / (2.0 * PRIOR_VAR) + 0.5 * (v_ * v_), 0.0)
    e_part = jnp.sum(sq, axis=(0, 1), keepdims=True)
    first = jnp.where((rowid >= cut) & (lax.broadcasted_iota(jnp.int32, (hs, LANE), 1) == 0),
                      w2b[...] * w2b[...] / (2.0 * PRIOR_VAR) + 0.5 * (m2b[...] * m2b[...]), 0.0)
    e_w2 = jnp.sum(first, axis=(0, 1), keepdims=True)
    loss = jnp.zeros((8, LANE), f32)
    for b in range(nshard):
        zt = ztot[b]
        loss = loss + (jnp.maximum(zt, 0.0) + jnp.log1p(jnp.exp(-jnp.abs(zt))) - ybuf[b].astype(f32) * zt)
    e_loss = jnp.sum(loss, axis=(0, 1), keepdims=True)
    e_part = e_part + jnp.where(rpos == 0, e_w2, 0.0) + jnp.where(zpos == 0, e_loss, 0.0)

    def as_row(ref):
        diag = jnp.where(rowid == lax.broadcasted_iota(jnp.int32, (hs, LANE), 1), ref[...], 0.0)
        return jnp.broadcast_to(jnp.sum(diag, axis=0, keepdims=True), (8, LANE))

    misc = jnp.where(sub8 == 0, as_row(w2b), jnp.where(sub8 == 1, as_row(m2b), jnp.broadcast_to(e_part, (8, LANE))))

    fin[0, q, zpos, rpos, 0:urows, :] = pos[...]
    fin[1, q, zpos, rpos, 0:urows, :] = mom[...]
    for arr in range(2):
        fin[arr, q, zpos, rpos, urows:urows + 8, :] = misc
    for make in (fin_ring, fin_cross):
        for arr in range(2):
            for d in range(1, side):
                make(arr, d).start()
        for arr in range(2):
            for d in range(1, side):
                make(arr, d).wait()
    for arr in range(2):
        fin_pair(arr).start()
    for arr in range(2):
        fin_pair(arr).wait()
    outs = []
    for arr, ref in ((0, fin_w), (1, fin_m)):
        for ch in range(2):
            for z in range(side):
                r0 = min(z * hs, hidden - hs)
                for i in range(nrow):
                    for k in range(nfull):
                        o, j = unit_at(i * nfull + k)
                        obuf[arr, ch, r0 + i * PACK:r0 + (i + 1) * PACK, k * LANE:(k + 1) * LANE] = fin[arr, ch, z, o, j:j + PACK, :]
                o, j = unit_at(nunit - 1)
                left = fin[arr, ch, z, o, j:j + PACK, :]
                for i in range(nrow):
                    v = pltpu.roll(left, LANE - i * rem, 1) if i else left
                    obuf[arr, ch, r0 + i * PACK:r0 + (i + 1) * PACK, nfull * LANE:feat] = v[:, 0:rem]
        cp = pltpu.make_async_copy(obuf.at[arr], ref, osem.at[arr])
        cp.start()
        outs.append(cp)
    for ch in range(2):
        for z in range(side):
            for r in range(side):
                misc_ref[ch, z, r] = fin[1, ch, z, r, urows:urows + 8, :]
    for cp in outs:
        cp.wait()


def solution(mesh):
    row_spec = P('data', None)
    label_spec = P('data')
    in_spec = P(None, 'parts', None)
    out_spec = P('parts', None)
    chain_spec = P('parts')
    side = math.isqrt(mesh.shape['data'] // 2)

    def run_chains(feats, labels, w_in, w_out, mom_in, mom_out):
        num_rows, feat = feats.shape
        hidden = w_in.shape[2]
        step = 1.0 / math.sqrt(num_rows * (feat + hidden))

        def device_body(x_rows, y_rows, pos_in, pos_out, vel_in, vel_out):
            rows = x_rows.shape[0]
            chains = pos_out.shape[0]
            hs = -(-(hidden // PACK) // side) * PACK
            kpad = -(-feat // LANE) * LANE
            nshard = 2 * side
            nfull = feat // LANE
            nunit = (hs // PACK) * nfull + 1
            urows = -(-nunit // side) * PACK
            groups = 4
            f32, bf16 = jnp.float32, jnp.bfloat16
            dma = pltpu.SemaphoreType.DMA
            vm = pltpu.VMEM
            cfg = (side, hidden, feat, rows, hs, step)
            full = jax.ShapeDtypeStruct((chains, hidden, feat), f32)
            any_spec = pl.BlockSpec(memory_space=pl.ANY)
            vmem_spec = pl.BlockSpec(memory_space=pltpu.VMEM)
            end_w, end_m, misc = pl.pallas_call(
                functools.partial(_kernel, cfg),
                out_shape=(full, full, jax.ShapeDtypeStruct((chains, side, side, 8, LANE), f32)),
                in_specs=[any_spec, vmem_spec, any_spec, any_spec, vmem_spec, vmem_spec],
                out_specs=(any_spec, any_spec, vmem_spec),
                scratch_shapes=[
                    vm((kpad, nshard * rows), bf16),
                    vm((nshard * rows, kpad), bf16),
                    vm((nshard, 8, rows // 8), jnp.int32),
                    vm((2, hs, feat), f32),
                    vm((hs, kpad), bf16),
                    vm((nshard, hs, rows), f32),
                    vm((nshard // groups, hs, rows), bf16),
                    vm((hs, kpad), f32),
                    vm((hs, LANE), f32),
                    vm((side, urows + 8, LANE), f32),
                    vm((side, urows + 8, LANE), f32),
                    vm((urows, LANE), f32),
                    vm((urows, LANE), f32),
                    vm((hs, LANE), f32),
                    vm((hs, LANE), f32),
                    vm((hs, LANE), f32),
                    vm((side, urows, LANE), bf16),
                    vm((2, side, nshard, 8, LANE), f32),
                    vm((nshard, 8, LANE), f32),
                    vm((2, chains, side, side, urows + 8, LANE), f32),
                    vm((2, chains, hidden, feat), f32),
                    dma((3,)), dma((7,)), dma((7,)), dma((7,)), dma((7,)),
                    dma((2, groups, side)), dma((2, groups, side)),
                    dma((side,)), dma((side,)), dma((side,)), dma((side,)),
                    dma((2, 2 * side)), dma((2, 2 * side)), dma((2,)),
                ],
                compiler_params=pltpu.CompilerParams(collective_id=0, has_side_effects=True, vmem_limit_bytes=67043328),
            )(x_rows.T, y_rows.reshape(8, rows // 8), pos_in.transpose(1, 2, 0), vel_in.transpose(1, 2, 0), pos_out, vel_out)
            keep = [misc[:, z, 0, 0:2, z * hs - min(z * hs, hidden - hs):hs] for z in range(side)]
            flat = jnp.concatenate(keep, axis=2)
            energy = jnp.sum(misc[:, :, :, 2, 0], axis=(1, 2))
            return end_w.transpose(2, 0, 1), flat[:, 0], end_m.transpose(2, 0, 1), flat[:, 1], energy

        mapped = jax.shard_map(device_body, mesh=mesh, in_specs=(row_spec, label_spec, in_spec, out_spec, in_spec, out_spec), out_specs=(in_spec, out_spec, in_spec, out_spec, chain_spec), check_vma=False)
        return mapped(feats, labels, w_in, w_out, mom_in, mom_out)

    return run_chains
```

time: 2080 us -> 387 us (0.19)
  waiting for transfers between devices: 848 us -> 0 us
  blocking collectives: 793 us -> 0 us
  Pallas kernels: 0 us -> 377 us
  other arithmetic: 191 us -> 1.61 us
  local copies, waits for them, and re-layouts: 133 us -> 8.09 us
  matrix products: 92.8 us -> 0 us
    psum x17 -> x0, waiting for transfers between devices: 847 us -> none  [log_post_grad(): grad_in, grad_out = lax.psum((grad_in, grad_out), 'data')]
    psum x17 -> x0, blocking collectives: 793 us -> none  [log_post_grad(): grad_in, grad_out = lax.psum((grad_in, grad_out), 'data')]
    pallas_call x0 -> x1, Pallas kernels: none -> 377 us  [device_body(): pl.pallas_call(functools.partial(_kernel, cfg), out_shape=(full, full, ja...]
    dot_general x34 -> x0, matrix products: 92.8 us -> none  [the longest x17 61.1 us: local_terms(): lax.dot_general(x_rows, back_grad.reshape(num_rows, num_chain * hidden),...]
    add x48 -> x0, other arithmetic: 90.3 us -> none  [the longest x15 84.8 us: leap_step(): vel_in + step_size * grad_in]
    dot_general x17 -> x0, local copies, waits for them, and re-layouts: 68.6 us -> none  [local_terms(): lax.dot_general(x_rows, back_grad.reshape(num_rows, num_chain * hidden),...]
    reduce_sum x38 -> x1, other arithmetic: 51.9 us -> 1.53 us  [device_body(): energy = jnp.sum(misc[:, :, :, 2, 0], axis=(1, 2))]
    while x120 -> x0, local copies, waits for them, and re-layouts: 48.9 us -> none
  transfers between devices with their start and end apart: 17 -> 0, of which waited for: 17 -> 0; matrix products, arithmetic and copies ran while one was open for 2% -> 0% of each run, Pallas kernels for 0% -> 0%
where the time goes in v1:
time: 387 us
  Pallas kernels  377 us (97%)
  local copies, waits for them, and re-layouts  8.09 us (2%)
    pallas_call x1, Pallas kernels, device_body(): pl.pallas_call(functools.partial(_kernel, cfg), out_shape=(full, full, ja...  377 us

profile of v1, /device:TPU:97, one launch (start us, length us, event | category | flops | bytes accessed | tf_op | source)
XLA Modules:
  0.0 387.0 jit_solution(4805818867050753250)
XLA Ops:
  0.6 376.7 %shard_map.101 = (f32[2,400,784]{2,1,0:T(8,128)}, f32[2,400,784]{2,1,0:T(8,128)}, f32[2,4,4,8,128]{4,3,2,1,0:T(8,128)}) custom-call(bf16[784,1024]{1,0:T(8,128)(2,1)} %bitcast.22, s32[8,128]{1,0:T(8,128)} %bitcast.23, f32[2,400,784]{2,1,0:T(8,128)} %bitcast.20, f32[2,400,784]{2,1,0:T(8,128)} %bitcast.21, f32[2,400]{1,0:T(2,128)} %wo_ref.1, f32[2,400]{1,0:T(2,128)} %mo_ref.1), custom_call_target="tpu_custom_call" | custom-call | tf_op jit(solution)/shard_map/pallas_call | solution.py:393
  377.3 0.7 slice_bitcast_fusion.1
  378.1 0.8 slice_bitcast_fusion.2
  378.8 0.7 slice_bitcast_fusion.3
  379.5 0.1 pad_maximum_fusion
  379.6 0.6 copy_bitcast_fusion
  380.2 1.5 slice_reduce_fusion
  381.7 0.0 copy-start
  381.8 3.7 copy.21
  385.5 0.0 copy-done
  385.5 1.6 copy.22
  (1 shorter events, 0.0 us)
Async XLA Ops:
  381.7 3.7 copy-start

commit v2 on v1

--- a/solution.py
+++ b/solution.py
@@ -15,9 +15,10 @@
 MESH_ID = pl.DeviceIdType.MESH
 
 
-def _kernel(cfg, xt_hbm, lab_ref, w_hbm, m_hbm, wo_ref, mo_ref, fin_w, fin_m, misc_ref,
+def _kernel(cfg, xt_hbm, lab_ref, w_hbm, m_hbm, wo_ref, mo_ref, fin,
             xt, x, ybuf, wload, wb, abuf, bbuf, gacc, g2acc, gsend, rsbuf, pos, mom, w2b, m2b, w2z, wag, zbuf, ztot,
-            fin, obuf, lsem, isend, irecv, ysend, yrecv, zsend, zrecv, rsend, rrecv, asend, arecv, fsend, frecv, osem):
+            lsem, isend, irecv, ysend, yrecv, zsend, zrecv, rsend, rrecv, asend, arecv, fsend, frecv,
+            csend, crecv, psend, precv):
     side, hidden, feat, rows, hs, step = cfg
     half = side // 2
     nshard = 2 * side
@@ -65,10 +66,14 @@
     own_slot = 2 * zpos + q
     par_slot = 2 * zpos + (1 - q)
 
-    def xcols(slot):
-        return xt.at[pl.ds(0, feat), pl.ds(pl.multiple_of(slot * rows, rows), rows)]
-
-    load_x = pltpu.make_async_copy(xt_hbm, xcols(own_slot), lsem.at[0])
+    parts = isend.shape[1]
+    piece = rows // parts
+    order = [d for d in range(1, side) if d == half] + [d for d in range(1, side) if d != half]
+
+    def xcols(slot, h):
+        return xt.at[pl.ds(0, feat), pl.ds(pl.multiple_of(slot * rows + h * piece, piece), piece)]
+
+    load_x = pltpu.make_async_copy(xt_hbm, xt.at[pl.ds(0, feat), pl.ds(pl.multiple_of(own_slot * rows, rows), rows)], lsem.at[0])
     load_w = pltpu.make_async_copy(w_hbm.at[q, pl.ds(start, hs), :], wload.at[0], lsem.at[1])
     load_m = pltpu.make_async_copy(m_hbm.at[q, pl.ds(start, hs), :], wload.at[1], lsem.at[2])
     load_x.start()
@@ -80,16 +85,25 @@
         pl.semaphore_signal(barrier, inc=1, device_id=dev, device_id_type=MESH_ID)
     pl.semaphore_wait(barrier, 2 * side - 1)
 
-    def ship(i, slot, dslot, dev):
-        cx = remote(xcols(slot), xcols(dslot), isend.at[i], irecv.at[i], dev)
-        cy = remote(ybuf.at[slot], ybuf.at[dslot], ysend.at[i], yrecv.at[i], dev)
-        cx.start()
-        cy.start()
-        return cx, cy
-
-    def landed(pair):
-        pair[0].wait_recv()
-        pair[1].wait_recv()
+    class Ship:
+        def __init__(self, i, slot, dslot, dev):
+            self.x = [remote(xcols(slot, h), xcols(dslot, h), isend.at[i, h], irecv.at[i, h], dev) for h in range(parts)]
+            self.y = remote(ybuf.at[slot], ybuf.at[dslot], ysend.at[i], yrecv.at[i], dev)
+
+        def start(self, h):
+            self.x[h].start()
+            if h == parts - 1:
+                self.y.start()
+
+        def landed(self, h):
+            self.x[h].wait_recv()
+            if h == parts - 1:
+                self.y.wait_recv()
+
+        def sent(self):
+            for c in self.x:
+                c.wait_send()
+            self.y.wait_send()
 
     def turn(slot):
         def body(t, _):
@@ -99,12 +113,20 @@
         lax.fori_loop(0, rows // LANE, body, 0)
 
     ybuf[own_slot] = lab_ref[...]
-    xt[pl.ds(feat, kpad - feat), :] = jnp.zeros((kpad - feat, nshard * rows), bf16)
+    up, down, far = (zpos + 1) % side, (zpos + side - 1) % side, (zpos + 2) % side
+    forth, back = zpeer[1], zpeer[side - 1]
+    s0 = Ship(0, own_slot, 2 * rpos + q, partner)
+    s1 = Ship(1, own_slot, own_slot, forth)
+    s2 = Ship(2, par_slot, par_slot, forth)
+    s3 = Ship(3, 2 * down + q, 2 * down + q, forth)
+    s4 = Ship(4, own_slot, own_slot, back)
+    s5 = Ship(5, par_slot, par_slot, back)
+    s6 = Ship(6, 2 * up + (1 - q), 2 * up + (1 - q), back)
     load_x.wait()
-    up, down, far = (zpos + 1) % side, (zpos + side - 1) % side, (zpos + 2) % side
-    s0 = ship(0, own_slot, 2 * rpos + q, partner)
-    s1 = ship(1, own_slot, own_slot, zpeer[1])
-    s4 = ship(4, own_slot, own_slot, zpeer[side - 1])
+    for h in range(parts):
+        for ship in (s0, s1, s4):
+            ship.start(h)
+    xt[feat:kpad, :] = jnp.zeros((kpad - feat, nshard * rows), bf16)
     turn(own_slot)
 
     lane = lax.broadcasted_iota(jnp.int32, (PACK, LANE), 1)
@@ -154,29 +176,54 @@
     column(wo_ref, w2b)
     column(mo_ref, m2b)
 
-    landed(s0)
-    s2 = ship(2, par_slot, par_slot, zpeer[1])
-    s5 = ship(5, par_slot, par_slot, zpeer[side - 1])
+    rowid = lax.broadcasted_iota(jnp.int32, (hs, LANE), 0)
+
+    def hidden_block(par, b, off):
+        for n in range(rows // 256):
+            pre = jnp.dot(wb[...], xt[:, pl.ds(off + n * 256, 256)], preferred_element_type=f32)
+            act = jnp.tanh(pre)
+            abuf[b, :, n * 256:(n + 1) * 256] = act
+            for h in range(2):
+                part = jnp.sum(act[:, h * LANE:(h + 1) * LANE] * w2z[...], axis=0, keepdims=True)
+                zbuf[par, zpos, b, 2 * n + h:2 * n + h + 1, :] = part
+
+    def first_pass(slot):
+        hidden_block(0, slot, pl.multiple_of(slot * rows, rows))
+
+    w2z[...] = jnp.where(rowid >= cut, w2b[...], 0.0)
+    for h in range(parts):
+        s0.landed(h)
+        s2.start(h)
+        s5.start(h)
     turn(par_slot)
-    landed(s1)
-    s3 = ship(3, 2 * down + q, 2 * down + q, zpeer[1])
+    first_pass(own_slot)
+    first_pass(par_slot)
+    for h in range(parts):
+        s1.landed(h)
+        s3.start(h)
     turn(2 * down + q)
-    landed(s4)
+    first_pass(2 * down + q)
+    for h in range(parts):
+        s4.landed(h)
     turn(2 * up + q)
-    landed(s5)
-    s6 = ship(6, 2 * up + (1 - q), 2 * up + (1 - q), zpeer[side - 1])
+    first_pass(2 * up + q)
+    for h in range(parts):
+        s5.landed(h)
+        s6.start(h)
     turn(2 * up + (1 - q))
-    landed(s2)
+    first_pass(2 * up + (1 - q))
+    for h in range(parts):
+        s2.landed(h)
     turn(2 * down + (1 - q))
-    landed(s3)
+    first_pass(2 * down + (1 - q))
+    for h in range(parts):
+        s3.landed(h)
     turn(2 * far + q)
-    landed(s6)
+    first_pass(2 * far + q)
+    for h in range(parts):
+        s6.landed(h)
     turn(2 * far + (1 - q))
-    for pair in (s0, s1, s2, s3, s4, s5, s6):
-        pair[0].wait_send()
-        pair[1].wait_send()
-
-    rowid = lax.broadcasted_iota(jnp.int32, (hs, LANE), 0)
+    first_pass(2 * far + (1 - q))
 
     def z_copy(par, g, d):
         block = pl.ds(g * per_group, per_group)
@@ -190,45 +237,52 @@
         return remote(wag.at[rpos], wag.at[rpos], asend.at[d], arecv.at[d], rpeer[d])
 
     def fin_ring(arr, d):
-        return remote(fin.at[arr, q, zpos, rpos], fin.at[arr, q, zpos, rpos],
-                      fsend.at[arr, d], frecv.at[arr, d], rpeer[d])
-
-    def fin_cross(arr, d):
-        return remote(fin.at[arr, q, zpos], fin.at[arr, q, zpos],
-                      fsend.at[arr, side + d], frecv.at[arr, side + d], zpeer[d])
-
-    def fin_pair(arr):
-        return remote(fin.at[arr, q], fin.at[arr, q], fsend.at[arr, 0], frecv.at[arr, 0], partner)
+        return remote(fin.at[arr, q, zpos, rpos], fin.at[arr, q, zpos, rpos], fsend.at[arr, d], frecv.at[arr, d], rpeer[d])
+
+    def fin_cross(arr, e, d):
+        block = fin.at[arr, q, zpos, (rpos + e) % side]
+        return remote(block, block, csend.at[arr, e, d], crecv.at[arr, e, d], zpeer[d])
+
+    def fin_pair(arr, w):
+        block = fin.at[arr, q, (zpos + w) % side]
+        return remote(block, block, psend.at[arr, w], precv.at[arr, w], partner)
+
+    def spread(arr):
+        for d in order:
+            fin_ring(arr, d).start()
+        for d in order:
+            fin_cross(arr, 0, d).start()
+
+    def relay(arr):
+        for d in reversed(order):
+            fin_ring(arr, d).wait_recv()
+            for dd in order:
+                fin_cross(arr, side - d, dd).start()
+
+    def over(arr):
+        fin_pair(arr, 0).start()
+        for w in reversed(order):
+            for e in range(side):
+                fin_cross(arr, e, side - w).wait_recv()
+            fin_pair(arr, w).start()
+
+    for g in range(groups):
+        for d in order:
+            z_copy(0, g, d).start()
+    for ship in (s0, s1, s2, s3, s4, s5, s6):
+        ship.sent()
 
     def gradient(k, _):
         par = k % 2
-        w2z[...] = jnp.where(rowid >= cut, w2b[...], 0.0)
-
-        def forward(g, _):
-            for bb in range(per_group):
-                b = g * per_group + bb
-                off = pl.multiple_of(b * rows, rows)
-                for n in range(rows // 256):
-                    pre = jnp.dot(wb[...], xt[:, pl.ds(off + n * 256, 256)], preferred_element_type=f32)
-                    act = jnp.tanh(pre)
-                    abuf[b, :, n * 256:(n + 1) * 256] = act
-                    for h in range(2):
-                        part = jnp.sum(act[:, h * LANE:(h + 1) * LANE] * w2z[...], axis=0, keepdims=True)
-                        zbuf[par, zpos, b, 2 * n + h:2 * n + h + 1, :] = part
-            for d in range(1, side):
-                z_copy(par, g, d).start()
-            return 0
-
-        lax.fori_loop(0, groups, forward, 0)
         gacc[...] = jnp.zeros_like(gacc)
         g2acc[...] = jnp.zeros_like(g2acc)
 
-        def backward(g, _):
+        def backward(g):
             for d in range(1, side):
                 z_copy(par, g, d).wait_recv()
             for bb in range(per_group):
                 b = g * per_group + bb
-                off = pl.multiple_of(b * rows, rows)
+                off = b * rows
                 logit = zbuf[par, 0, b]
                 for s in range(1, side):
                     logit = logit + zbuf[par, s, b]
@@ -239,10 +293,12 @@
                     rr = jnp.broadcast_to(res[n:n + 1, :], (hs, LANE))
                     g2acc[...] += rr * act
                     bbuf[bb, :, n * LANE:(n + 1) * LANE] = ((rr * w2b[...]) * (1.0 - act * act)).astype(bf16)
-                gacc[...] += jnp.dot(bbuf[bb], x[pl.ds(off, rows), :], preferred_element_type=f32)
-            return 0
-
-        lax.fori_loop(0, groups, backward, 0)
+                for lo in range(0, kpad, 256):
+                    hi = min(lo + 256, kpad)
+                    gacc[:, lo:hi] += jnp.dot(bbuf[bb], x[off:off + rows, lo:hi], preferred_element_type=f32)
+
+        for g in range(groups):
+            backward(g)
         pack(gacc, gsend, LANE)
         g2 = jnp.zeros((8, LANE), f32)
         for i in range(hs // 8):
@@ -250,7 +306,7 @@
             g2 = jnp.where(lane8 == i, jnp.broadcast_to(col, (8, LANE)), g2)
         for o in range(side):
             gsend[o, urows:urows + 8, :] = g2
-        for d in range(1, side):
+        for d in order:
             r_copy(d).start()
         rsbuf[rpos] = gsend[rpos]
         for g in range(groups):
@@ -275,8 +331,15 @@
             pos[...] = pos[...] + step * mom[...]
             w2b[...] = w2b[...] + step * m2b[...]
             wag[rpos] = pos[...].astype(bf16)
-            for d in range(1, side):
+            for d in order:
                 a_copy(d).start()
+
+            @pl.when(k == LEAPS - 1)
+            def _():
+                fin[0, q, zpos, rpos, 0:urows, :] = pos[...]
+                fin[0, q, zpos, rpos, urows:urows + 8, :] = jnp.zeros((8, LANE), f32)
+                spread(0)
+
             for d in range(1, side):
                 a_copy(d).wait_recv()
             for i in range(nrow):
@@ -288,8 +351,18 @@
             for i in range(nrow):
                 v = pltpu.roll(left, LANE - i * rem, 1) if i else left
                 wb[i * PACK:(i + 1) * PACK, nfull * LANE:] = jnp.where(lane < rem, v, 0.0).astype(bf16)
+            w2z[...] = jnp.where(rowid >= cut, w2b[...], 0.0)
+            for g in range(groups):
+                for b in range(g * per_group, (g + 1) * per_group):
+                    hidden_block(1 - par, b, b * rows)
+                for d in order:
+                    z_copy(1 - par, g, d).start()
             for d in range(1, side):
                 a_copy(d).wait_send()
+
+            @pl.when(k == LEAPS - 1)
+            def _():
+                relay(0)
 
         return 0
 
@@ -320,43 +393,70 @@
 
     misc = jnp.where(sub8 == 0, as_row(w2b), jnp.where(sub8 == 1, as_row(m2b), jnp.broadcast_to(e_part, (8, LANE))))
 
-    fin[0, q, zpos, rpos, 0:urows, :] = pos[...]
     fin[1, q, zpos, rpos, 0:urows, :] = mom[...]
+    fin[1, q, zpos, rpos, urows:urows + 8, :] = misc
+    spread(1)
+    over(0)
+    relay(1)
+    over(1)
     for arr in range(2):
-        fin[arr, q, zpos, rpos, urows:urows + 8, :] = misc
-    for make in (fin_ring, fin_cross):
-        for arr in range(2):
-            for d in range(1, side):
-                make(arr, d).start()
-        for arr in range(2):
-            for d in range(1, side):
-                make(arr, d).wait()
-    for arr in range(2):
-        fin_pair(arr).start()
-    for arr in range(2):
-        fin_pair(arr).wait()
-    outs = []
-    for arr, ref in ((0, fin_w), (1, fin_m)):
-        for ch in range(2):
+        for w in range(side):
+            fin_pair(arr, w).wait()
+        for d in order:
+            fin_ring(arr, d).wait_send()
+            for e in range(side):
+                fin_cross(arr, e, d).wait_send()
+
+
+def _unpack(cfg, packed, end_w, end_m, w_row, m_row, energy, fin, obuf, lsem, sem):
+    side, hidden, feat, rows, hs, step = cfg
+    chains = fin.shape[1]
+    nfull = feat // LANE
+    rem = feat - nfull * LANE
+    nrow = hs // PACK
+    nunit = nrow * nfull + 1
+    own = -(-nunit // side)
+    urows = own * PACK
+    f32 = jnp.float32
+    copies = []
+    loads = {(arr, ch): pltpu.make_async_copy(packed.at[arr, ch], fin.at[arr, ch], lsem.at[arr, ch]) for arr in range(2) for ch in range(chains)}
+    for ld in loads.values():
+        ld.start()
+    for arr, ref in ((0, end_w), (1, end_m)):
+        for ch in range(chains):
+            loads[arr, ch].wait()
             for z in range(side):
                 r0 = min(z * hs, hidden - hs)
                 for i in range(nrow):
+                    r1 = r0 + i * PACK
                     for k in range(nfull):
-                        o, j = unit_at(i * nfull + k)
-                        obuf[arr, ch, r0 + i * PACK:r0 + (i + 1) * PACK, k * LANE:(k + 1) * LANE] = fin[arr, ch, z, o, j:j + PACK, :]
-                o, j = unit_at(nunit - 1)
-                left = fin[arr, ch, z, o, j:j + PACK, :]
+                        u = i * nfull + k
+                        obuf[arr, ch, r1:r1 + PACK, k * LANE:(k + 1) * LANE] = fin[arr, ch, z, u // own, (u % own) * PACK:(u % own + 1) * PACK, :]
+                u = nunit - 1
+                left = fin[arr, ch, z, u // own, (u % own) * PACK:(u % own + 1) * PACK, :]
                 for i in range(nrow):
                     v = pltpu.roll(left, LANE - i * rem, 1) if i else left
                     obuf[arr, ch, r0 + i * PACK:r0 + (i + 1) * PACK, nfull * LANE:feat] = v[:, 0:rem]
-        cp = pltpu.make_async_copy(obuf.at[arr], ref, osem.at[arr])
-        cp.start()
-        outs.append(cp)
-    for ch in range(2):
+            cp = pltpu.make_async_copy(obuf.at[arr, ch], ref.at[ch], sem.at[arr, ch])
+            cp.start()
+            copies.append(cp)
+    width = -(-hidden // LANE) * LANE
+    lane = lax.broadcasted_iota(jnp.int32, (8, width), 1)
+    for ch in range(chains):
+        acc = jnp.zeros((8, width), f32)
+        tot = jnp.zeros((8, LANE), f32)
         for z in range(side):
+            tile = fin[1, ch, z, 0, urows:urows + 8, :]
+            wide = jnp.concatenate([tile, jnp.zeros((8, width - LANE), f32)], axis=1)
+            r0 = min(z * hs, hidden - hs)
+            wide = pltpu.roll(wide, r0, 1) if r0 else wide
+            acc = jnp.where((lane >= z * hs) & (lane < (z + 1) * hs), wide, acc)
             for r in range(side):
-                misc_ref[ch, z, r] = fin[1, ch, z, r, urows:urows + 8, :]
-    for cp in outs:
+                tot = tot + fin[1, ch, z, r, urows:urows + 8, :]
+        w_row[ch:ch + 1, :] = acc[0:1, 0:hidden]
+        m_row[ch:ch + 1, :] = acc[1:2, 0:hidden]
+        energy[ch] = jnp.sum(tot[2:3, 0:1])
+    for cp in copies:
         cp.wait()
 
 
@@ -390,11 +490,12 @@
             full = jax.ShapeDtypeStruct((chains, hidden, feat), f32)
             any_spec = pl.BlockSpec(memory_space=pl.ANY)
             vmem_spec = pl.BlockSpec(memory_space=pltpu.VMEM)
-            end_w, end_m, misc = pl.pallas_call(
+            piece_shape = (2, chains, side, side, urows + 8, LANE)
+            fin = pl.pallas_call(
                 functools.partial(_kernel, cfg),
-                out_shape=(full, full, jax.ShapeDtypeStruct((chains, side, side, 8, LANE), f32)),
+                out_shape=jax.ShapeDtypeStruct(piece_shape, f32),
                 in_specs=[any_spec, vmem_spec, any_spec, any_spec, vmem_spec, vmem_spec],
-                out_specs=(any_spec, any_spec, vmem_spec),
+                out_specs=vmem_spec,
                 scratch_shapes=[
                     vm((kpad, nshard * rows), bf16),
                     vm((nshard * rows, kpad), bf16),
@@ -415,19 +516,24 @@
                     vm((side, urows, LANE), bf16),
                     vm((2, side, nshard, 8, LANE), f32),
                     vm((nshard, 8, LANE), f32),
-                    vm((2, chains, side, side, urows + 8, LANE), f32),
-                    vm((2, chains, hidden, feat), f32),
-                    dma((3,)), dma((7,)), dma((7,)), dma((7,)), dma((7,)),
+                    dma((3,)), dma((7, 2)), dma((7, 2)), dma((7,)), dma((7,)),
                     dma((2, groups, side)), dma((2, groups, side)),
                     dma((side,)), dma((side,)), dma((side,)), dma((side,)),
-                    dma((2, 2 * side)), dma((2, 2 * side)), dma((2,)),
+                    dma((2, side)), dma((2, side)), dma((2, side, side)), dma((2, side, side)),
+                    dma((2, side)), dma((2, side)),
                 ],
                 compiler_params=pltpu.CompilerParams(collective_id=0, has_side_effects=True, vmem_limit_bytes=67043328),
             )(x_rows.T, y_rows.reshape(8, rows // 8), pos_in.transpose(1, 2, 0), vel_in.transpose(1, 2, 0), pos_out, vel_out)
-            keep = [misc[:, z, 0, 0:2, z * hs - min(z * hs, hidden - hs):hs] for z in range(side)]
-            flat = jnp.concatenate(keep, axis=2)
-            energy = jnp.sum(misc[:, :, :, 2, 0], axis=(1, 2))
-            return end_w.transpose(2, 0, 1), flat[:, 0], end_m.transpose(2, 0, 1), flat[:, 1], energy
+            end_w, end_m, w_row, m_row, energy = pl.pallas_call(
+                functools.partial(_unpack, cfg),
+                out_shape=(full, full, jax.ShapeDtypeStruct((chains, hidden), f32), jax.ShapeDtypeStruct((chains, hidden), f32),
+                           jax.ShapeDtypeStruct((chains,), f32)),
+                in_specs=[any_spec],
+                out_specs=(any_spec, any_spec, vmem_spec, vmem_spec, pl.BlockSpec(memory_space=pltpu.SMEM)),
+                scratch_shapes=[vm(piece_shape, f32), vm((2, chains, hidden, feat), f32), dma((2, chains)), dma((2, chains))],
+                compiler_params=pltpu.CompilerParams(vmem_limit_bytes=67043328),
+            )(fin)
+            return end_w.transpose(2, 0, 1), w_row, end_m.transpose(2, 0, 1), m_row, energy
 
         mapped = jax.shard_map(device_body, mesh=mesh, in_specs=(row_spec, label_spec, in_spec, out_spec, in_spec, out_spec), out_specs=(in_spec, out_spec, in_spec, out_spec, chain_spec), check_vma=False)
         return mapped(feats, labels, w_in, w_out, mom_in, mom_out)

time: 387 us -> 353 us (0.912)
  Pallas kernels: 377 us -> 352 us
  local copies, waits for them, and re-layouts: 8.09 us -> 0 us
    pallas_call x1 -> x2, Pallas kernels: 377 us -> 352 us  [the longest x1 346 us: device_body(): pl.pallas_call(functools.partial(_kernel, cfg), out_shape=jax.ShapeDtypeS...]
    unnamed x5 -> x0, local copies, waits for them, and re-layouts: 5.89 us -> none
where the time goes in v2:
time: 353 us; the launch traced here: 352 us
  Pallas kernels  352 us (100%)
    pallas_call x1, Pallas kernels, device_body(): pl.pallas_call(functools.partial(_kernel, cfg), out_shape=jax.ShapeDtypeS...  346 us

profile of v2, /device:TPU:97, one launch (start us, length us, event | category | flops | bytes accessed | tf_op | source)
XLA Modules:
  0.0 352.5 jit_solution(16133731057199911320)
XLA Ops:
  0.6 346.5 %shard_map.101.packed = f32[2,2,4,4,184,128]{5,4,3,2,1,0:T(8,128)} custom-call(bf16[784,1024]{1,0:T(8,128)(2,1)} %bitcast.8, s32[8,128]{1,0:T(8,128)} %bitcast.9, f32[2,400,784]{2,1,0:T(8,128)} %bitcast.6, f32[2,400,784]{2,1,0:T(8,128)} %bitcast.7, f32[2,400]{1,0:T(2,128)} %wo_ref.1, f32[2,400]{1,0:T(2,128)} %mo_ref.1), custom_call_target="tpu_custom_call" | custom-call | tf_op jit(solution)/shard_map/pallas_call | solution.py:494
  347.1 5.4 %shard_map.102 = (f32[2,400,784]{2,1,0:T(8,128)}, f32[2,400,784]{2,1,0:T(8,128)}, f32[2,400]{1,0:T(2,128)}, f32[2,400]{1,0:T(2,128)}, f32[2]{0:T(128)}) custom-call(f32[2,2,4,4,184,128]{5,4,3,2,1,0:T(8,128)} %shard_map.101.packed), custom_call_target="tpu_custom_call" | custom-call | tf_op jit(solution)/shard_map/pallas_call | solution.py:527

commit v3 on v2

v3 whole, which is shorter than its diff:
```python
import functools
import math

import jax
import jax.numpy as jnp
from jax import lax
from jax.experimental import pallas as pl
from jax.experimental.pallas import tpu as pltpu
from jax.sharding import PartitionSpec as P

LEAPS = 16
PRIOR_VAR = 1.0
LANE = 128
MESH_ID = pl.DeviceIdType.MESH


class Tiles:
    def __init__(self, side, feat, hs):
        self.nrow = hs // 8
        self.nfull = feat // LANE
        self.rem = feat - self.nfull * LANE
        self.per = LANE // self.rem
        split = 2 * (self.nfull // 3)
        self.lanes = split * LANE
        left = [(None, j) for j in range(-(-self.nrow // self.per))]
        self.part = [[(i, k) for i in range(self.nrow) for k in range(split)],
                     [(i, k) for i in range(self.nrow) for k in range(split, self.nfull)] + left]
        self.count = [len(p) // side for p in self.part]
        assert all(len(p) % side == 0 for p in self.part)
        self.size = [8 * n for n in self.count]

    def value(self, src, tile):
        i, k = tile
        if i is not None:
            return src[8 * i:8 * i + 8, k * LANE:(k + 1) * LANE]
        acc = None
        for g in range(min(self.per, self.nrow - k * self.per)):
            i = k * self.per + g
            v = src[8 * i:8 * i + 8, self.nfull * LANE:src.shape[1]]
            if v.shape[1] < LANE:
                v = jnp.concatenate([v, jnp.zeros((8, LANE - v.shape[1]), v.dtype)], axis=1)
            v = pltpu.roll(v, g * self.rem, 1) if g else v
            acc = v if acc is None else acc + v
        return acc


def _kernel(cfg, xt_hbm, lab_hbm, w_hbm, m_hbm, wo_hbm, mo_hbm, fin,
            xt, x, ybuf, oload, estage, g2sum, wload, wb, abuf, bbuf, gacc, g2acc, gsend_a, gsend_b, rsum_a, rsum_b, pos, mom, w2b, m2b, w2z,
            wag_a, wag_b, zbuf, ztot,
            lsem, isend, irecv, ysend, yrecv, zsend, zrecv, rsend, rrecv, asend, arecv, fsend, frecv,
            csend, crecv, psend, precv):
    side, hidden, feat, rows, hs, step, sizes = cfg
    half = side // 2
    nshard = 2 * side
    tiles = Tiles(side, feat, hs)
    nfull, rem = tiles.nfull, tiles.rem
    size_a, size_b = tiles.size
    urows = size_a + size_b
    gsend, rsum, wag = (gsend_a, gsend_b), (rsum_a, rsum_b), (wag_a, wag_b)
    span = (slice(0, size_a), slice(size_a, urows))
    kpad = xt.shape[0]
    nlt = rows // LANE
    groups = len(sizes)
    blocks = [range(sum(sizes[:g]), sum(sizes[:g + 1])) for g in range(groups)]
    f32, bf16 = jnp.float32, jnp.bfloat16

    me = lax.axis_index('data')
    core = me % 2
    xx = (me // 2) % side
    yy = me // (2 * side)

    def fold(y, x_):
        return (x_ // half + y // half) % 2

    q = (core + fold(yy, xx)) % 2
    zpos = xx * (1 - q) + yy * q
    rpos = yy * (1 - q) + xx * q

    def device(z, r, role):
        x2 = z * (1 - role) + r * role
        y2 = r * (1 - role) + z * role
        return {'data': (y2 * side + x2) * 2 + (role + fold(y2, x2)) % 2}

    zpeer = [device((zpos + d) % side, rpos, q) for d in range(side)]
    rpeer = [device(zpos, (rpos + d) % side, q) for d in range(side)]
    partner = device(rpos, zpos, 1 - q)

    def remote(src, dst, ssem, rsem, dev):
        return pltpu.make_async_remote_copy(src_ref=src, dst_ref=dst, send_sem=ssem, recv_sem=rsem,
                                            device_id=dev, device_id_type=MESH_ID)

    start = jnp.minimum(zpos * hs, hidden - hs)
    start = pl.multiple_of(start, 8)
    cut = zpos * hs - start

    own_slot = 2 * zpos + q
    par_slot = 2 * zpos + (1 - q)

    parts = isend.shape[1]
    piece = rows // parts
    order = [d for d in range(1, side) if d == half] + [d for d in range(1, side) if d != half]

    def xcols(slot, h):
        return xt.at[pl.ds(0, feat), pl.ds(pl.multiple_of(slot * rows + h * piece, piece), piece)]

    load_x = [pltpu.make_async_copy(xt_hbm.at[:, pl.ds(h * piece, piece)], xcols(own_slot, h), lsem.at[2 + h]) for h in range(parts)]
    load_w = pltpu.make_async_copy(w_hbm.at[q, pl.ds(start, hs), :], wload.at[0], lsem.at[0])
    load_m = pltpu.make_async_copy(m_hbm.at[q, pl.ds(start, hs), :], wload.at[1], lsem.at[1])
    load_y = pltpu.make_async_copy(lab_hbm, ybuf.at[own_slot], ysend.at[7])
    load_o = [pltpu.make_async_copy(src, oload.at[i], yrecv.at[7 + i]) for i, src in enumerate((wo_hbm, mo_hbm))]
    for cp in load_x + [load_y, load_w, load_m] + load_o:
        cp.start()

    barrier = pltpu.get_barrier_semaphore()
    for dev in zpeer[1:] + rpeer[1:] + [partner]:
        pl.semaphore_signal(barrier, inc=1, device_id=dev, device_id_type=MESH_ID)
    pl.semaphore_wait(barrier, 2 * side - 1)

    class Ship:
        def __init__(self, i, slot, dslot, dev):
            self.x = [remote(xcols(slot, h), xcols(dslot, h), isend.at[i, h], irecv.at[i, h], dev) for h in range(parts)]
            self.y = remote(ybuf.at[slot], ybuf.at[dslot], ysend.at[i], yrecv.at[i], dev)

        def start(self, h):
            self.x[h].start()
            if h == parts - 1:
                self.y.start()

        def landed(self, h):
            self.x[h].wait_recv()
            if h == parts - 1:
                self.y.wait_recv()

        def sent(self):
            for c in self.x:
                c.wait_send()
            self.y.wait_send()

    def turn(slot, h):
        def body(t, _):
            off = pl.multiple_of(slot * rows + h * piece + t * LANE, LANE)
            x[pl.ds(off, LANE), :] = xt[:, pl.ds(off, LANE)].T
            return 0
        lax.fori_loop(0, piece // LANE, body, 0)

    up, down, far = (zpos + 1) % side, (zpos + side - 1) % side, (zpos + 2) % side
    forth, back = zpeer[1], zpeer[side - 1]
    s0 = Ship(0, own_slot, 2 * rpos + q, partner)
    s1 = Ship(1, own_slot, own_slot, forth)
    s2 = Ship(2, par_slot, par_slot, forth)
    s3 = Ship(3, 2 * down + q, 2 * down + q, forth)
    s4 = Ship(4, own_slot, own_slot, back)
    s5 = Ship(5, par_slot, par_slot, back)
    s6 = Ship(6, 2 * up + (1 - q), 2 * up + (1 - q), back)
    load_y.wait()
    for h in range(parts):
        load_x[h].wait()
        for ship in (s0, s1, s4):
            ship.start(h)
    xt[feat:kpad, :] = jnp.zeros((kpad - feat, nshard * rows), bf16)
    for h in range(parts):
        turn(own_slot, h)

    lane8 = lax.broadcasted_iota(jnp.int32, (8, LANE), 1)
    sub8 = lax.broadcasted_iota(jnp.int32, (8, LANE), 0)

    def pack(p, src):
        n = tiles.count[p]
        for t, tile in enumerate(tiles.part[p]):
            gsend[p][t // n, 8 * (t % n):8 * (t % n) + 8, :] = tiles.value(src, tile)

    def adopt(p, src):
        n = tiles.count[p]
        held = [src[o].astype(f32) for o in range(side)]
        got = {tile: held[t // n][8 * (t % n):8 * (t % n) + 8] for t, tile in enumerate(tiles.part[p])}
        for k in sorted({k for i, k in tiles.part[p] if i is not None}):
            for i in range(0, tiles.nrow, 2):
                v = got[i, k] if i + 1 == tiles.nrow else jnp.concatenate([got[i, k], got[i + 1, k]], axis=0)
                wb[8 * i:8 * i + v.shape[0], k * LANE:(k + 1) * LANE] = v.astype(bf16)
        if (None, 0) in got:
            def left(i):
                g = i % tiles.per
                v = got[None, i // tiles.per]
                v = pltpu.roll(v, LANE - g * rem, 1) if g else v
                return jnp.where(lane8 < rem, v, 0.0)
            for i in range(0, tiles.nrow, 2):
                v = left(i) if i + 1 == tiles.nrow else jnp.concatenate([left(i), left(i + 1)], axis=0)
                wb[8 * i:8 * i + v.shape[0], nfull * LANE:] = v.astype(bf16)

    load_w.wait()
    load_m.wait()
    for src, dst in ((1, mom), (0, pos)):
        for p in range(2):
            pack(p, wload.at[src])
            dst[span[p], :] = gsend[p][rpos, 0:tiles.size[p], :]
    wb[:, nfull * LANE:] = jnp.zeros((hs, kpad - nfull * LANE), bf16)
    wb[:, 0:feat] = wload[0].astype(bf16)

    def column(ref, dst):
        width = -(-hidden // LANE) * LANE
        v = jnp.concatenate([oload[ref, pl.ds(q, 1), :], jnp.zeros((1, width - hidden), f32)], axis=1)
        lanes = lax.broadcasted_iota(jnp.int32, (8, width), 1)
        subs = lax.broadcasted_iota(jnp.int32, (8, width), 0)
        v = jnp.broadcast_to(v, (8, width))
        for i in range(hs // 8):
            hit = jnp.where(lanes == start + i * 8 + subs, v, 0.0)
            dst[i * 8:(i + 1) * 8, :] = jnp.broadcast_to(jnp.sum(hit, axis=1, keepdims=True), (8, LANE))

    for cp in load_o:
        cp.wait()
    column(0, w2b)
    column(1, m2b)

    rowid = lax.broadcasted_iota(jnp.int32, (hs, LANE), 0)

    def hidden_block(par, b, off, first, last, done=0):
        for n in range(first, last):
            pre = jnp.dot(wb[:, done:], xt[done:, pl.ds(off + n * 256, 256)], preferred_element_type=f32)
            if done:
                pre = pre + abuf[b, :, n * 256:(n + 1) * 256]
            act = jnp.tanh(pre)
            abuf[b, :, n * 256:(n + 1) * 256] = act
            for h in range(2):
                part = jnp.sum(act[:, h * LANE:(h + 1) * LANE] * w2z[...], axis=0, keepdims=True)
                zbuf[par, zpos, b, 2 * n + h:2 * n + h + 1, :] = part

    def hidden_start(b, off):
        for n in range(rows // 256):
            abuf[b, :, n * 256:(n + 1) * 256] = jnp.dot(wb[:, 0:tiles.lanes], xt[0:tiles.lanes, pl.ds(off + n * 256, 256)],
                                                        preferred_element_type=f32)

    def first_pass(slot, h):
        per = piece // 256
        hidden_block(0, slot, pl.multiple_of(slot * rows, rows), h * per, (h + 1) * per)

    def take(slot, h):
        turn(slot, h)
        first_pass(slot, h)

    w2z[...] = jnp.where(rowid >= cut, w2b[...], 0.0)
    for h in range(parts):
        s0.landed(h)
        s2.start(h)
        s5.start(h)
    for h in range(parts):
        take(par_slot, h)
        first_pass(own_slot, h)
    for h in range(parts):
        s1.landed(h)
        s3.start(h)
        take(2 * down + q, h)
    for h in range(parts):
        s4.landed(h)
        take(2 * up + q, h)
    for h in range(parts):
        s5.landed(h)
        s6.start(h)
        take(2 * up + (1 - q), h)
    for h in range(parts):
        s2.landed(h)
        take(2 * down + (1 - q), h)
    for h in range(parts):
        s3.landed(h)
        take(2 * far + q, h)
        s6.landed(h)
        take(2 * far + (1 - q), h)

    def z_copy(par, g, d):
        block = pl.ds(blocks[g][0], sizes[g])
        return remote(zbuf.at[par, zpos, block], zbuf.at[par, zpos, block],
                      zsend.at[par, g, d], zrecv.at[par, g, d], zpeer[d])

    def r_copy(p, d):
        return remote(gsend[p].at[(rpos + d) % side], rsum[p].at[rpos], rsend.at[p, d], rrecv.at[p, d], rpeer[d])

    def a_copy(p, d):
        return remote(wag[p].at[rpos], wag[p].at[rpos], asend.at[p, d], arecv.at[p, d], rpeer[d])

    def fin_ring(arr, d):
        return remote(fin.at[arr, q, zpos, rpos], fin.at[arr, q, zpos, rpos], fsend.at[arr, d], frecv.at[arr, d], rpeer[d])

    def fin_cross(arr, e, d):
        block = fin.at[arr, q, zpos, (rpos + e) % side]
        return remote(block, block, csend.at[arr, e, d], crecv.at[arr, e, d], zpeer[d])

    def fin_pair(arr, w):
        block = fin.at[arr, q, (zpos + w) % side]
        return remote(block, block, psend.at[arr, w], precv.at[arr, w], partner)

    def spread(arr):
        for d in order:
            fin_ring(arr, d).start()
        for d in order:
            fin_cross(arr, 0, d).start()

    def relay(arr):
        for d in reversed(order):
            fin_ring(arr, d).wait_recv()
            for dd in order:
                fin_cross(arr, side - d, dd).start()

    def over(arr):
        fin_pair(arr, 0).start()
        for w in reversed(order):
            for e in range(side):
                fin_cross(arr, e, side - w).wait_recv()
            fin_pair(arr, w).start()

    for g in range(groups):
        for d in order:
            z_copy(0, g, d).start()
    for ship in (s0, s1, s2, s3, s4, s5, s6):
        ship.sent()

    def squares(main, out):
        low = cut // 8
        sq = jnp.zeros((8, LANE), f32)
        for p in range(2):
            n = tiles.count[p]
            wide = len({k for i, k in tiles.part[p] if i is not None})
            mains = tiles.nrow * wide
            for j in range(n):
                t = n * rpos + j
                v = main[span[p].start + 8 * j:span[p].start + 8 * j + 8, :]
                tile_row = jnp.where(t < mains, t // wide + 0 * lane8, (t - mains) * tiles.per + lane8 // rem)
                sq = sq + jnp.where(tile_row >= low, v * v, 0.0)
        for i in range(tiles.nrow):
            v = out[8 * i:8 * i + 8, :]
            sq = sq + jnp.where((i >= low) & (rpos == 0) & (lane8 == 0), v * v, 0.0)
        return sq

    def gradient(k, _):
        par = k % 2

        def weigh(g):
            for d in range(1, side):
                z_copy(par, g, d).wait_recv()
            for bb, b in enumerate(blocks[g]):
                logit = zbuf[par, 0, b]
                for s in range(1, side):
                    logit = logit + zbuf[par, s, b]
                ztot[b] = logit
                res = ybuf[b].astype(f32) - jax.nn.sigmoid(logit)
                for n in range(nlt):
                    act = abuf[b, :, n * LANE:(n + 1) * LANE]
                    rr = jnp.broadcast_to(res[n:n + 1, :], (hs, LANE))
                    part = rr * act
                    g2acc[...] = part if b == 0 and n == 0 else g2acc[...] + part
                    bbuf[bb, :, n * LANE:(n + 1) * LANE] = ((rr * w2b[...]) * (1.0 - act * act)).astype(bf16)

        def contract(g, first, last):
            for bb, b in enumerate(blocks[g]):
                for lo in range(first, last, 256):
                    hi = min(lo + 256, last)
                    prod = jnp.dot(bbuf[bb], x[b * rows:(b + 1) * rows, lo:hi], preferred_element_type=f32)
                    gacc[:, lo:hi] = prod if b == 0 else gacc[:, lo:hi] + prod

        for g in range(groups - 1):
            weigh(g)
            contract(g, 0, kpad)
        weigh(groups - 1)
        contract(groups - 1, 0, tiles.lanes)
        pack(0, gacc)
        for d in order:
            r_copy(0, d).start()
        contract(groups - 1, tiles.lanes, kpad)
        g2 = jnp.zeros((8, LANE), f32)
        for i in range(hs // 8):
            col = jnp.sum(g2acc[i * 8:(i + 1) * 8, :], axis=1, keepdims=True)
            g2 = jnp.where(lane8 == i, jnp.broadcast_to(col, (8, LANE)), g2)
        for o in range(side):
            gsend_b[o, size_b:size_b + 8, :] = g2
        pack(1, gacc)
        for d in order:
            r_copy(1, d).start()
        for p in range(2):
            rsum[p][rpos] = gsend[p][rpos]
        for g in range(groups):
            for d in range(1, side):
                z_copy(par, g, d).wait_send()
        coef = jnp.where((k == 0) | (k == LEAPS), 0.5 * step, step).astype(f32)

        def kick(p):
            for d in range(1, side):
                r_copy(p, d).wait_recv()
            total = rsum[p][0]
            for s in range(1, side):
                total = total + rsum[p][s]
            mom[span[p], :] = mom[span[p], :] + coef * (total[0:tiles.size[p]] - pos[span[p], :] / PRIOR_VAR)
            if p == 1:
                g2sum[...] = total[size_b:size_b + 8]

        def kick_out():
            tile = g2sum[...]
            for i in range(hs // 8):
                blk = slice(i * 8, (i + 1) * 8)
                gcol = jnp.broadcast_to(tile[:, i:i + 1], (8, LANE))
                m2b[blk, :] = m2b[blk, :] + coef * (gcol - w2b[blk, :] / PRIOR_VAR)

        @pl.when(k < LEAPS)
        def _():
            for p in range(2):
                kick(p)
                pos[span[p], :] = pos[span[p], :] + step * mom[span[p], :]
                wag[p][rpos] = pos[span[p], :].astype(bf16)
                for d in order:
                    a_copy(p, d).start()
            kick_out()
            w2b[...] = w2b[...] + step * m2b[...]
            w2z[...] = jnp.where(rowid >= cut, w2b[...], 0.0)

            @pl.when(k == LEAPS - 1)
            def _():
                fin[0, q, zpos, rpos, 0:urows, :] = pos[...]
                fin[0, q, zpos, rpos, urows:urows + 8, :] = jnp.zeros((8, LANE), f32)
                spread(0)

            for p in range(2):
                for d in range(1, side):
                    r_copy(p, d).wait_send()
            for p in range(2):
                for d in range(1, side):
                    a_copy(p, d).wait_recv()
                adopt(p, wag[p])
                if p == 0:
                    for b in blocks[0]:
                        hidden_start(b, b * rows)
            for g in range(groups):
                for b in blocks[g]:
                    hidden_block(1 - par, b, b * rows, 0, rows // 256, tiles.lanes if g == 0 else 0)
                for d in order:
                    z_copy(1 - par, g, d).start()
            for p in range(2):
                for d in range(1, side):
                    a_copy(p, d).wait_send()

            @pl.when(k == LEAPS - 1)
            def _():
                relay(0)

        @pl.when(k == LEAPS)
        def _():
            loss = jnp.zeros((8, LANE), f32)
            for b in range(nshard):
                zt = ztot[b]
                loss = loss + (jnp.maximum(zt, 0.0) + jnp.log1p(jnp.exp(-jnp.abs(zt))) - ybuf[b].astype(f32) * zt)
            estage[...] = jnp.where(zpos == 0, loss, 0.0) + squares(pos, w2b) / (2.0 * PRIOR_VAR)
            for p in range(2):
                kick(p)
            kick_out()
            for p in range(2):
                for d in range(1, side):
                    r_copy(p, d).wait_send()

        return 0

    lax.fori_loop(0, LEAPS + 1, gradient, 0)

    def as_row(ref):
        diag = jnp.where(rowid == lax.broadcasted_iota(jnp.int32, (hs, LANE), 1), ref[...], 0.0)
        return jnp.broadcast_to(jnp.sum(diag, axis=0, keepdims=True), (8, LANE))

    share = jnp.sum(estage[...] + 0.5 * squares(mom, m2b), axis=0, keepdims=True)
    misc = jnp.where(sub8 == 0, as_row(w2b), jnp.where(sub8 == 1, as_row(m2b), jnp.broadcast_to(share, (8, LANE))))

    fin[1, q, zpos, rpos, 0:urows, :] = mom[...]
    fin[1, q, zpos, rpos, urows:urows + 8, :] = misc
    spread(1)
    over(0)
    relay(1)
    over(1)
    for arr in range(2):
        for w in range(side):
            fin_pair(arr, w).wait()
        for d in order:
            fin_ring(arr, d).wait_send()
            for e in range(side):
                fin_cross(arr, e, d).wait_send()


def _unpack(cfg, fin, end_w, end_m, w_out, m_out, e_out, obuf, w_row, m_row, energy, sem, tail):
    side, hidden, feat, rows, hs, step, sizes = cfg
    chains = fin.shape[1]
    tiles = Tiles(side, feat, hs)
    base = (0, tiles.size[0])
    urows = tiles.size[0] + tiles.size[1]
    f32 = jnp.float32
    width = -(-hidden // LANE) * LANE
    lane = lax.broadcasted_iota(jnp.int32, (8, width), 1)
    for ch in range(chains):
        acc = jnp.zeros((8, width), f32)
        tot = jnp.zeros((8, LANE), f32)
        for z in range(side):
            tile = fin[1, ch, z, 0, urows:urows + 8, :]
            wide = jnp.concatenate([tile, jnp.zeros((8, width - LANE), f32)], axis=1)
            r0 = min(z * hs, hidden - hs)
            wide = pltpu.roll(wide, r0, 1) if r0 else wide
            acc = jnp.where((lane >= z * hs) & (lane < (z + 1) * hs), wide, acc)
            for r in range(side):
                tot = tot + fin[1, ch, z, r, urows:urows + 8, :]
        w_row[ch:ch + 1, :] = acc[0:1, 0:hidden]
        m_row[ch:ch + 1, :] = acc[1:2, 0:hidden]
        energy[ch] = jnp.sum(tot[2:3, :])
    copies = [pltpu.make_async_copy(src, dst, tail.at[i]) for i, (src, dst) in enumerate(((w_row, w_out), (m_row, m_out), (energy, e_out)))]
    for cp in copies:
        cp.start()
    for arr, ref in ((0, end_w), (1, end_m)):
        for ch in range(chains):
            for z in range(side):
                r0 = min(z * hs, hidden - hs)
                for p in range(2):
                    n = tiles.count[p]
                    for t, (i, k) in enumerate(tiles.part[p]):
                        at = base[p] + 8 * (t % n)
                        tile = fin[arr, ch, z, t // n, at:at + 8, :]
                        if i is not None:
                            obuf[arr, ch, r0 + 8 * i:r0 + 8 * i + 8, k * LANE:(k + 1) * LANE] = tile
                            continue
                        for g in range(min(tiles.per, tiles.nrow - k * tiles.per)):
                            r1 = r0 + 8 * (k * tiles.per + g)
                            v = pltpu.roll(tile, LANE - g * tiles.rem, 1) if g else tile
                            obuf[arr, ch, r1:r1 + 8, tiles.nfull * LANE:feat] = v[:, 0:tiles.rem]
            cp = pltpu.make_async_copy(obuf.at[arr, ch], ref.at[ch], sem.at[arr, ch])
            cp.start()
            copies.append(cp)
    for cp in copies:
        cp.wait()


def solution(mesh):
    row_spec = P('data', None)
    label_spec = P('data')
    in_spec = P(None, 'parts', None)
    out_spec = P('parts', None)
    chain_spec = P('parts')
    side = math.isqrt(mesh.shape['data'] // 2)

    def run_chains(feats, labels, w_in, w_out, mom_in, mom_out):
        num_rows, feat = feats.shape
        hidden = w_in.shape[2]
        step = 1.0 / math.sqrt(num_rows * (feat + hidden))

        def device_body(x_rows, y_rows, pos_in, pos_out, vel_in, vel_out):
            rows = x_rows.shape[0]
            chains = pos_out.shape[0]
            hs = -(-(hidden // 8) // side) * 8
            kpad = -(-feat // LANE) * LANE
            nshard = 2 * side
            size_a, size_b = Tiles(side, feat, hs).size
            urows = size_a + size_b
            sizes = (2, 3, 3)
            pieces = 4
            groups = len(sizes)
            f32, bf16 = jnp.float32, jnp.bfloat16
            dma = pltpu.SemaphoreType.DMA
            vm = pltpu.VMEM
            cfg = (side, hidden, feat, rows, hs, step, sizes)
            full = jax.ShapeDtypeStruct((chains, hidden, feat), f32)
            any_spec = pl.BlockSpec(memory_space=pl.ANY)
            vmem_spec = pl.BlockSpec(memory_space=pltpu.VMEM)
            hbm_spec = pl.BlockSpec(memory_space=pltpu.HBM)
            piece_shape = (2, chains, side, side, urows + 8, LANE)
            fin = pl.pallas_call(
                functools.partial(_kernel, cfg),
                out_shape=vm(piece_shape, f32),
                in_specs=[hbm_spec] * 6,
                out_specs=vmem_spec,
                scratch_shapes=[
                    vm((kpad, nshard * rows), bf16),
                    vm((nshard * rows, kpad), bf16),
                    vm((nshard, 8, rows // 8), jnp.int32),
                    vm((2, chains, hidden), f32),
                    vm((8, LANE), f32),
                    vm((8, LANE), f32),
                    vm((2, hs, feat), f32),
                    vm((hs, kpad), bf16),
                    vm((nshard, hs, rows), f32),
                    vm((max(sizes), hs, rows), bf16),
                    vm((hs, kpad), f32),
                    vm((hs, LANE), f32),
                    vm((side, size_a, LANE), f32),
                    vm((side, size_b + 8, LANE), f32),
                    vm((side, size_a, LANE), f32),
                    vm((side, size_b + 8, LANE), f32),
                    vm((urows, LANE), f32),
                    vm((urows, LANE), f32),
                    vm((hs, LANE), f32),
                    vm((hs, LANE), f32),
                    vm((hs, LANE), f32),
                    vm((side, size_a, LANE), bf16),
                    vm((side, size_b, LANE), bf16),
                    vm((2, side, nshard, 8, LANE), f32),
                    vm((nshard, 8, LANE), f32),
                    dma((2 + pieces,)), dma((7, pieces)), dma((7, pieces)), dma((8,)), dma((9,)),
                    dma((2, groups, side)), dma((2, groups, side)),
                    dma((2, side)), dma((2, side)), dma((2, side)), dma((2, side)),
                    dma((2, side)), dma((2, side)), dma((2, side, side)), dma((2, side, side)),
                    dma((2, side)), dma((2, side)),
                ],
                compiler_params=pltpu.CompilerParams(collective_id=0, has_side_effects=True, vmem_limit_bytes=67043328 - 4 * math.prod(piece_shape)),
            )(x_rows.T, y_rows.reshape(8, rows // 8), pos_in.transpose(1, 2, 0), vel_in.transpose(1, 2, 0), pos_out, vel_out)
            end_w, end_m, w_row, m_row, energy = pl.pallas_call(
                functools.partial(_unpack, cfg),
                out_shape=(full, full, jax.ShapeDtypeStruct((chains, hidden), f32), jax.ShapeDtypeStruct((chains, hidden), f32),
                           jax.ShapeDtypeStruct((chains,), f32)),
                in_specs=[vmem_spec],
                out_specs=(any_spec,) * 5,
                scratch_shapes=[vm((2, chains, hidden, feat), f32), vm((chains, hidden), f32), vm((chains, hidden), f32),
                                pltpu.SMEM((chains,), f32), dma((2, chains)), dma((3,))],
                compiler_params=pltpu.CompilerParams(vmem_limit_bytes=16 << 20),
            )(fin)
            return end_w.transpose(2, 0, 1), w_row, end_m.transpose(2, 0, 1), m_row, energy

        mapped = jax.shard_map(device_body, mesh=mesh, in_specs=(row_spec, label_spec, in_spec, out_spec, in_spec, out_spec), out_specs=(in_spec, out_spec, in_spec, out_spec, chain_spec), check_vma=False)
        return mapped(feats, labels, w_in, w_out, mom_in, mom_out)

    return run_chains
```

time: 353 us -> 321 us (0.909)
  Pallas kernels: 352 us -> 320 us
    pallas_call x1, Pallas kernels: 346 us -> 317 us  [device_body(): pl.pallas_call(functools.partial(_kernel, cfg), out_shape=vm(piece_shape,...]
where the time goes in v3:
time: 321 us
  Pallas kernels  320 us (100%)
    pallas_call x1, Pallas kernels, device_body(): pl.pallas_call(functools.partial(_kernel, cfg), out_shape=vm(piece_shape,...  317 us

profile of v3, /device:TPU:97, one launch (start us, length us, event | category | flops | bytes accessed | tf_op | source)
XLA Modules:
  0.0 321.0 jit_solution(12727544248654523277)
XLA Ops:
  0.6 317.5 %shard_map.101.fin = f32[2,2,4,4,168,128]{5,4,3,2,1,0:T(8,128)S(1)} custom-call(bf16[784,1024]{1,0:T(8,128)(2,1)} %bitcast.8, s32[8,128]{1,0:T(8,128)} %bitcast.9, f32[2,400,784]{2,1,0:T(8,128)} %bitcast.6, f32[2,400,784]{2,1,0:T(8,128)} %bitcast.7, f32[2,400]{1,0:T(2,128)} %wo_hbm.1, f32[2,400]{1,0:T(2,128)} %mo_hbm.1), custom_call_target="tpu_custom_call" | custom-call | tf_op jit(solution)/shard_map/pallas_call | solution.py:563
  318.1 2.7 shard_map.102

commit v4 on v3

--- a/solution.py
+++ b/solution.py
@@ -11,6 +11,7 @@
 LEAPS = 16
 PRIOR_VAR = 1.0
 LANE = 128
+BEGIN = 6
 MESH_ID = pl.DeviceIdType.MESH
 
 
@@ -39,14 +40,19 @@
             v = src[8 * i:8 * i + 8, self.nfull * LANE:src.shape[1]]
             if v.shape[1] < LANE:
                 v = jnp.concatenate([v, jnp.zeros((8, LANE - v.shape[1]), v.dtype)], axis=1)
-            v = pltpu.roll(v, g * self.rem, 1) if g else v
+                v = pltpu.roll(v, g * self.rem, 1) if g else v
+            else:
+                v = jnp.where(self.group() == g, v, 0.0)
             acc = v if acc is None else acc + v
         return acc
 
+    def group(self):
+        return lax.broadcasted_iota(jnp.int32, (8, LANE), 1) // self.rem
+
 
 def _kernel(cfg, xt_hbm, lab_hbm, w_hbm, m_hbm, wo_hbm, mo_hbm, fin,
             xt, x, ybuf, oload, estage, g2sum, wload, wb, abuf, bbuf, gacc, g2acc, gsend_a, gsend_b, rsum_a, rsum_b, pos, mom, w2b, m2b, w2z,
-            wag_a, wag_b, zbuf, ztot,
+            wag_a, zbuf, ztot,
             lsem, isend, irecv, ysend, yrecv, zsend, zrecv, rsend, rrecv, asend, arecv, fsend, frecv,
             csend, crecv, psend, precv):
     side, hidden, feat, rows, hs, step, sizes = cfg
@@ -56,10 +62,11 @@
     nfull, rem = tiles.nfull, tiles.rem
     size_a, size_b = tiles.size
     urows = size_a + size_b
-    gsend, rsum, wag = (gsend_a, gsend_b), (rsum_a, rsum_b), (wag_a, wag_b)
-    span = (slice(0, size_a), slice(size_a, urows))
+    full_b = side * size_b
+    span = (slice(0, size_a), slice(size_a, size_a + full_b))
     kpad = xt.shape[0]
     nlt = rows // LANE
+    begin = BEGIN
     groups = len(sizes)
     blocks = [range(sum(sizes[:g]), sum(sizes[:g + 1])) for g in range(groups)]
     f32, bf16 = jnp.float32, jnp.bfloat16
@@ -139,6 +146,8 @@
     def turn(slot, h):
         def body(t, _):
             off = pl.multiple_of(slot * rows + h * piece + t * LANE, LANE)
+            for row in range(feat, kpad, rem):
+                xt[row:row + rem, pl.ds(off, LANE)] = xt[feat - rem:feat, pl.ds(off, LANE)]
             x[pl.ds(off, LANE), :] = xt[:, pl.ds(off, LANE)].T
             return 0
         lax.fori_loop(0, piece // LANE, body, 0)
@@ -157,7 +166,6 @@
         load_x[h].wait()
         for ship in (s0, s1, s4):
             ship.start(h)
-    xt[feat:kpad, :] = jnp.zeros((kpad - feat, nshard * rows), bf16)
     for h in range(parts):
         turn(own_slot, h)
 
@@ -167,22 +175,25 @@
     def pack(p, src):
         n = tiles.count[p]
         for t, tile in enumerate(tiles.part[p]):
-            gsend[p][t // n, 8 * (t % n):8 * (t % n) + 8, :] = tiles.value(src, tile)
+            if p == 0:
+                gsend_a[t // n, 8 * (t % n):8 * (t % n) + 8, :] = tiles.value(src, tile)
+            else:
+                gsend_b[8 * t:8 * t + 8, :] = tiles.value(src, tile)
 
     def adopt(p, src):
         n = tiles.count[p]
-        held = [src[o].astype(f32) for o in range(side)]
-        got = {tile: held[t // n][8 * (t % n):8 * (t % n) + 8] for t, tile in enumerate(tiles.part[p])}
+        if p == 0:
+            held = [src[o].astype(f32) for o in range(side)]
+            got = {tile: held[t // n][8 * (t % n):8 * (t % n) + 8] for t, tile in enumerate(tiles.part[p])}
+        else:
+            got = {tile: src[size_a + 8 * t:size_a + 8 * t + 8, :] for t, tile in enumerate(tiles.part[p])}
         for k in sorted({k for i, k in tiles.part[p] if i is not None}):
             for i in range(0, tiles.nrow, 2):
                 v = got[i, k] if i + 1 == tiles.nrow else jnp.concatenate([got[i, k], got[i + 1, k]], axis=0)
                 wb[8 * i:8 * i + v.shape[0], k * LANE:(k + 1) * LANE] = v.astype(bf16)
         if (None, 0) in got:
             def left(i):
-                g = i % tiles.per
-                v = got[None, i // tiles.per]
-                v = pltpu.roll(v, LANE - g * rem, 1) if g else v
-                return jnp.where(lane8 < rem, v, 0.0)
+                return jnp.where(tiles.group() == i % tiles.per, got[None, i // tiles.per], 0.0)
             for i in range(0, tiles.nrow, 2):
                 v = left(i) if i + 1 == tiles.nrow else jnp.concatenate([left(i), left(i + 1)], axis=0)
                 wb[8 * i:8 * i + v.shape[0], nfull * LANE:] = v.astype(bf16)
@@ -192,9 +203,10 @@
     for src, dst in ((1, mom), (0, pos)):
         for p in range(2):
             pack(p, wload.at[src])
-            dst[span[p], :] = gsend[p][rpos, 0:tiles.size[p], :]
-    wb[:, nfull * LANE:] = jnp.zeros((hs, kpad - nfull * LANE), bf16)
-    wb[:, 0:feat] = wload[0].astype(bf16)
+        dst[span[0], :] = gsend_a[rpos]
+        dst[span[1], :] = gsend_b[0:full_b]
+    adopt(0, gsend_a)
+    adopt(1, pos)
 
     def column(ref, dst):
         width = -(-hidden // LANE) * LANE
@@ -213,11 +225,15 @@
 
     rowid = lax.broadcasted_iota(jnp.int32, (hs, LANE), 0)
 
-    def hidden_block(par, b, off, first, last, done=0):
+    split = tiles.lanes
+
+    def hidden_block(par, b, off, first, last, begun=False):
         for n in range(first, last):
-            pre = jnp.dot(wb[:, done:], xt[done:, pl.ds(off + n * 256, 256)], preferred_element_type=f32)
-            if done:
-                pre = pre + abuf[b, :, n * 256:(n + 1) * 256]
+            cols = pl.ds(off + n * 256, 256)
+            if begun:
+                pre = jnp.dot(wb[:, 0:split], xt[0:split, cols], preferred_element_type=f32) + abuf[b, :, n * 256:(n + 1) * 256]
+            else:
+                pre = jnp.dot(wb[...], xt[:, cols], preferred_element_type=f32)
             act = jnp.tanh(pre)
             abuf[b, :, n * 256:(n + 1) * 256] = act
             for h in range(2):
@@ -226,7 +242,7 @@
 
     def hidden_start(b, off):
         for n in range(rows // 256):
-            abuf[b, :, n * 256:(n + 1) * 256] = jnp.dot(wb[:, 0:tiles.lanes], xt[0:tiles.lanes, pl.ds(off + n * 256, 256)],
+            abuf[b, :, n * 256:(n + 1) * 256] = jnp.dot(wb[:, split:], xt[split:, pl.ds(off + n * 256, 256)],
                                                         preferred_element_type=f32)
 
     def first_pass(slot, h):
@@ -270,11 +286,16 @@
         return remote(zbuf.at[par, zpos, block], zbuf.at[par, zpos, block],
                       zsend.at[par, g, d], zrecv.at[par, g, d], zpeer[d])
 
-    def r_copy(p, d):
-        return remote(gsend[p].at[(rpos + d) % side], rsum[p].at[rpos], rsend.at[p, d], rrecv.at[p, d], rpeer[d])
-
-    def a_copy(p, d):
-        return remote(wag[p].at[rpos], wag[p].at[rpos], asend.at[p, d], arecv.at[p, d], rpeer[d])
+    def r_copy(p, d, par):
+        if p == 0:
+            return remote(gsend_a.at[(rpos + d) % side], rsum_a.at[rpos], rsend.at[0, d], rrecv.at[0, d], rpeer[d])
+        return remote(gsend_b, rsum_b.at[par, rpos], rsend.at[1 + par, d], rrecv.at[1 + par, d], rpeer[d])
+
+    def a_copy(d):
+        return remote(wag_a.at[rpos], wag_a.at[rpos], asend.at[d], arecv.at[d], rpeer[d])
+
+    def own_share():
+        return pl.ds(pl.multiple_of(size_a + rpos * size_b, 8), size_b)
 
     def fin_ring(arr, d):
         return remote(fin.at[arr, q, zpos, rpos], fin.at[arr, q, zpos, rpos], fsend.at[arr, d], frecv.at[arr, d], rpeer[d])
@@ -321,7 +342,8 @@
             mains = tiles.nrow * wide
             for j in range(n):
                 t = n * rpos + j
-                v = main[span[p].start + 8 * j:span[p].start + 8 * j + 8, :]
+                at = 8 * j if p == 0 else pl.multiple_of(size_a + 8 * (n * rpos + j), 8)
+                v = main[pl.ds(at, 8), :]
                 tile_row = jnp.where(t < mains, t // wide + 0 * lane8, (t - mains) * tiles.per + lane8 // rem)
                 sq = sq + jnp.where(tile_row >= low, v * v, 0.0)
         for i in range(tiles.nrow):
@@ -335,7 +357,7 @@
         def weigh(g):
             for d in range(1, side):
                 z_copy(par, g, d).wait_recv()
-            for bb, b in enumerate(blocks[g]):
+            for b in blocks[g]:
                 logit = zbuf[par, 0, b]
                 for s in range(1, side):
                     logit = logit + zbuf[par, s, b]
@@ -346,35 +368,33 @@
                     rr = jnp.broadcast_to(res[n:n + 1, :], (hs, LANE))
                     part = rr * act
                     g2acc[...] = part if b == 0 and n == 0 else g2acc[...] + part
-                    bbuf[bb, :, n * LANE:(n + 1) * LANE] = ((rr * w2b[...]) * (1.0 - act * act)).astype(bf16)
+                    bbuf[b, :, n * LANE:(n + 1) * LANE] = ((rr * w2b[...]) * (1.0 - act * act)).astype(bf16)
 
         def contract(g, first, last):
-            for bb, b in enumerate(blocks[g]):
+            for b in blocks[g]:
                 for lo in range(first, last, 256):
                     hi = min(lo + 256, last)
-                    prod = jnp.dot(bbuf[bb], x[b * rows:(b + 1) * rows, lo:hi], preferred_element_type=f32)
+                    prod = jnp.dot(bbuf[b], x[b * rows:(b + 1) * rows, lo:hi], preferred_element_type=f32)
                     gacc[:, lo:hi] = prod if b == 0 else gacc[:, lo:hi] + prod
 
-        for g in range(groups - 1):
+        for g in range(groups):
             weigh(g)
-            contract(g, 0, kpad)
-        weigh(groups - 1)
-        contract(groups - 1, 0, tiles.lanes)
+            contract(g, 0, split)
         pack(0, gacc)
         for d in order:
-            r_copy(0, d).start()
-        contract(groups - 1, tiles.lanes, kpad)
+            r_copy(0, d, par).start()
         g2 = jnp.zeros((8, LANE), f32)
         for i in range(hs // 8):
             col = jnp.sum(g2acc[i * 8:(i + 1) * 8, :], axis=1, keepdims=True)
             g2 = jnp.where(lane8 == i, jnp.broadcast_to(col, (8, LANE)), g2)
-        for o in range(side):
-            gsend_b[o, size_b:size_b + 8, :] = g2
+        gsend_b[full_b:full_b + 8, :] = g2
+        for g in range(groups):
+            contract(g, split, kpad)
         pack(1, gacc)
         for d in order:
-            r_copy(1, d).start()
-        for p in range(2):
-            rsum[p][rpos] = gsend[p][rpos]
+            r_copy(1, d, par).start()
+        rsum_a[rpos] = gsend_a[rpos]
+        rsum_b[par, rpos] = gsend_b[...]
         for g in range(groups):
             for d in range(1, side):
                 z_copy(par, g, d).wait_send()
@@ -382,13 +402,15 @@
 
         def kick(p):
             for d in range(1, side):
-                r_copy(p, d).wait_recv()
-            total = rsum[p][0]
+                r_copy(p, d, par).wait_recv()
+            held = [rsum_a[s] if p == 0 else rsum_b[par, s] for s in range(side)]
+            total = held[0]
             for s in range(1, side):
-                total = total + rsum[p][s]
-            mom[span[p], :] = mom[span[p], :] + coef * (total[0:tiles.size[p]] - pos[span[p], :] / PRIOR_VAR)
+                total = total + held[s]
+            size = size_a if p == 0 else full_b
+            mom[span[p], :] = mom[span[p], :] + coef * (total[0:size] - pos[span[p], :] / PRIOR_VAR)
             if p == 1:
-                g2sum[...] = total[size_b:size_b + 8]
+                g2sum[...] = total[size:size + 8]
 
         def kick_out():
             tile = g2sum[...]
@@ -399,40 +421,40 @@
 
         @pl.when(k < LEAPS)
         def _():
-            for p in range(2):
-                kick(p)
-                pos[span[p], :] = pos[span[p], :] + step * mom[span[p], :]
-                wag[p][rpos] = pos[span[p], :].astype(bf16)
-                for d in order:
-                    a_copy(p, d).start()
+            kick(0)
+            pos[span[0], :] = pos[span[0], :] + step * mom[span[0], :]
+            wag_a[rpos] = pos[span[0], :].astype(bf16)
+            for d in order:
+                a_copy(d).start()
+            kick(1)
+            pos[span[1], :] = pos[span[1], :] + step * mom[span[1], :]
+            adopt(1, pos)
+            for b in range(begin):
+                hidden_start(b, b * rows)
             kick_out()
             w2b[...] = w2b[...] + step * m2b[...]
             w2z[...] = jnp.where(rowid >= cut, w2b[...], 0.0)
 
             @pl.when(k == LEAPS - 1)
             def _():
-                fin[0, q, zpos, rpos, 0:urows, :] = pos[...]
+                fin[0, q, zpos, rpos, 0:size_a, :] = pos[span[0], :]
+                fin[0, q, zpos, rpos, size_a:urows, :] = pos[own_share(), :]
                 fin[0, q, zpos, rpos, urows:urows + 8, :] = jnp.zeros((8, LANE), f32)
                 spread(0)
 
             for p in range(2):
                 for d in range(1, side):
-                    r_copy(p, d).wait_send()
-            for p in range(2):
-                for d in range(1, side):
-                    a_copy(p, d).wait_recv()
-                adopt(p, wag[p])
-                if p == 0:
-                    for b in blocks[0]:
-                        hidden_start(b, b * rows)
+                    r_copy(p, d, par).wait_send()
+            for d in range(1, side):
+                a_copy(d).wait_recv()
+            adopt(0, wag_a)
             for g in range(groups):
                 for b in blocks[g]:
-                    hidden_block(1 - par, b, b * rows, 0, rows // 256, tiles.lanes if g == 0 else 0)
+                    hidden_block(1 - par, b, b * rows, 0, rows // 256, b < begin)
                 for d in order:
                     z_copy(1 - par, g, d).start()
-            for p in range(2):
-                for d in range(1, side):
-                    a_copy(p, d).wait_send()
+            for d in range(1, side):
+                a_copy(d).wait_send()
 
             @pl.when(k == LEAPS - 1)
             def _():
@@ -450,7 +472,7 @@
             kick_out()
             for p in range(2):
                 for d in range(1, side):
-                    r_copy(p, d).wait_send()
+                    r_copy(p, d, par).wait_send()
 
         return 0
 
@@ -463,7 +485,8 @@
     share = jnp.sum(estage[...] + 0.5 * squares(mom, m2b), axis=0, keepdims=True)
     misc = jnp.where(sub8 == 0, as_row(w2b), jnp.where(sub8 == 1, as_row(m2b), jnp.broadcast_to(share, (8, LANE))))
 
-    fin[1, q, zpos, rpos, 0:urows, :] = mom[...]
+    fin[1, q, zpos, rpos, 0:size_a, :] = mom[span[0], :]
+    fin[1, q, zpos, rpos, size_a:urows, :] = mom[own_share(), :]
     fin[1, q, zpos, rpos, urows:urows + 8, :] = misc
     spread(1)
     over(0)
@@ -548,7 +571,7 @@
             nshard = 2 * side
             size_a, size_b = Tiles(side, feat, hs).size
             urows = size_a + size_b
-            sizes = (2, 3, 3)
+            sizes = (3, 3, 2)
             pieces = 4
             groups = len(sizes)
             f32, bf16 = jnp.float32, jnp.bfloat16
@@ -575,25 +598,24 @@
                     vm((2, hs, feat), f32),
                     vm((hs, kpad), bf16),
                     vm((nshard, hs, rows), f32),
-                    vm((max(sizes), hs, rows), bf16),
+                    vm((nshard, hs, rows), bf16),
                     vm((hs, kpad), f32),
                     vm((hs, LANE), f32),
                     vm((side, size_a, LANE), f32),
-                    vm((side, size_b + 8, LANE), f32),
+                    vm((side * size_b + 8, LANE), f32),
                     vm((side, size_a, LANE), f32),
-                    vm((side, size_b + 8, LANE), f32),
-                    vm((urows, LANE), f32),
-                    vm((urows, LANE), f32),
+                    vm((2, side, side * size_b + 8, LANE), f32),
+                    vm((size_a + side * size_b, LANE), f32),
+                    vm((size_a + side * size_b, LANE), f32),
                     vm((hs, LANE), f32),
                     vm((hs, LANE), f32),
                     vm((hs, LANE), f32),
                     vm((side, size_a, LANE), bf16),
-                    vm((side, size_b, LANE), bf16),
                     vm((2, side, nshard, 8, LANE), f32),
                     vm((nshard, 8, LANE), f32),
                     dma((2 + pieces,)), dma((7, pieces)), dma((7, pieces)), dma((8,)), dma((9,)),
                     dma((2, groups, side)), dma((2, groups, side)),
-                    dma((2, side)), dma((2, side)), dma((2, side)), dma((2, side)),
+                    dma((3, side)), dma((3, side)), dma((side,)), dma((side,)),
                     dma((2, side)), dma((2, side)), dma((2, side, side)), dma((2, side, side)),
                     dma((2, side)), dma((2, side)),
                 ],

time: 321 us -> 312 us (0.972)
  Pallas kernels: 320 us -> 311 us
    pallas_call x1, Pallas kernels: 317 us -> 308 us  [device_body(): pl.pallas_call(functools.partial(_kernel, cfg), out_shape=vm(piece_shape,...]
where the time goes in v4:
time: 312 us
  Pallas kernels  311 us (100%)
    pallas_call x1, Pallas kernels, device_body(): pl.pallas_call(functools.partial(_kernel, cfg), out_shape=vm(piece_shape,...  308 us

profile of v4, /device:TPU:97, one launch (start us, length us, event | category | flops | bytes accessed | tf_op | source)
XLA Modules:
  0.0 311.9 jit_solution(16935533814952161208)
XLA Ops:
  0.6 308.4 %shard_map.101.fin = f32[2,2,4,4,168,128]{5,4,3,2,1,0:T(8,128)S(1)} custom-call(bf16[784,1024]{1,0:T(8,128)(2,1)} %bitcast.8, s32[8,128]{1,0:T(8,128)} %bitcast.9, f32[2,400,784]{2,1,0:T(8,128)} %bitcast.6, f32[2,400,784]{2,1,0:T(8,128)} %bitcast.7, f32[2,400]{1,0:T(2,128)} %wo_hbm.1, f32[2,400]{1,0:T(2,128)} %mo_hbm.1), custom_call_target="tpu_custom_call" | custom-call | tf_op jit(solution)/shard_map/pallas_call | solution.py:586
  309.0 2.7 shard_map.102

commit v5 on v4

--- a/solution.py
+++ b/solution.py
@@ -63,6 +63,7 @@
     size_a, size_b = tiles.size
     urows = size_a + size_b
     full_b = side * size_b
+    head = size_a + 8
     span = (slice(0, size_a), slice(size_a, size_a + full_b))
     kpad = xt.shape[0]
     nlt = rows // LANE
@@ -294,25 +295,31 @@
     def a_copy(d):
         return remote(wag_a.at[rpos], wag_a.at[rpos], asend.at[d], arecv.at[d], rpeer[d])
 
-    def own_share():
-        return pl.ds(pl.multiple_of(size_a + rpos * size_b, 8), size_b)
-
     def fin_ring(arr, d):
-        return remote(fin.at[arr, q, zpos, rpos], fin.at[arr, q, zpos, rpos], fsend.at[arr, d], frecv.at[arr, d], rpeer[d])
+        block = fin.at[arr, q, zpos, rpos, 0:head]
+        return remote(block, block, fsend.at[arr, d], frecv.at[arr, d], rpeer[d])
 
     def fin_cross(arr, e, d):
-        block = fin.at[arr, q, zpos, (rpos + e) % side]
+        block = fin.at[arr, q, zpos, (rpos + e) % side, 0:head] if e < side else fin.at[arr, q, zpos, :, head:]
         return remote(block, block, csend.at[arr, e, d], crecv.at[arr, e, d], zpeer[d])
 
     def fin_pair(arr, w):
         block = fin.at[arr, q, (zpos + w) % side]
         return remote(block, block, psend.at[arr, w], precv.at[arr, w], partner)
+
+    def stage(arr, src, misc):
+        fin[arr, q, zpos, rpos, 0:size_a, :] = src[span[0], :]
+        fin[arr, q, zpos, rpos, size_a:head, :] = misc
+        for r in range(side):
+            fin[arr, q, zpos, r, head:, :] = src[size_a + r * size_b:size_a + (r + 1) * size_b, :]
 
     def spread(arr):
         for d in order:
             fin_ring(arr, d).start()
         for d in order:
             fin_cross(arr, 0, d).start()
+        for d in order:
+            fin_cross(arr, side, d).start()
 
     def relay(arr):
         for d in reversed(order):
@@ -323,7 +330,7 @@
     def over(arr):
         fin_pair(arr, 0).start()
         for w in reversed(order):
-            for e in range(side):
+            for e in range(side + 1):
                 fin_cross(arr, e, side - w).wait_recv()
             fin_pair(arr, w).start()
 
@@ -371,11 +378,13 @@
                     bbuf[b, :, n * LANE:(n + 1) * LANE] = ((rr * w2b[...]) * (1.0 - act * act)).astype(bf16)
 
         def contract(g, first, last):
-            for b in blocks[g]:
-                for lo in range(first, last, 256):
-                    hi = min(lo + 256, last)
-                    prod = jnp.dot(bbuf[b], x[b * rows:(b + 1) * rows, lo:hi], preferred_element_type=f32)
-                    gacc[:, lo:hi] = prod if b == 0 else gacc[:, lo:hi] + prod
+            for lo in range(first, last, 256):
+                hi = min(lo + 256, last)
+                prod = None
+                for b in (range(nshard) if g is None else blocks[g]):
+                    one = jnp.dot(bbuf[b], x[b * rows:(b + 1) * rows, lo:hi], preferred_element_type=f32)
+                    prod = one if prod is None else prod + one
+                gacc[:, lo:hi] = prod if not g else gacc[:, lo:hi] + prod
 
         for g in range(groups):
             weigh(g)
@@ -388,8 +397,7 @@
             col = jnp.sum(g2acc[i * 8:(i + 1) * 8, :], axis=1, keepdims=True)
             g2 = jnp.where(lane8 == i, jnp.broadcast_to(col, (8, LANE)), g2)
         gsend_b[full_b:full_b + 8, :] = g2
-        for g in range(groups):
-            contract(g, split, kpad)
+        contract(None, split, kpad)
         pack(1, gacc)
         for d in order:
             r_copy(1, d, par).start()
@@ -437,9 +445,7 @@
 
             @pl.when(k == LEAPS - 1)
             def _():
-                fin[0, q, zpos, rpos, 0:size_a, :] = pos[span[0], :]
-                fin[0, q, zpos, rpos, size_a:urows, :] = pos[own_share(), :]
-                fin[0, q, zpos, rpos, urows:urows + 8, :] = jnp.zeros((8, LANE), f32)
+                stage(0, pos, jnp.zeros((8, LANE), f32))
                 spread(0)
 
             for p in range(2):
@@ -485,9 +491,7 @@
     share = jnp.sum(estage[...] + 0.5 * squares(mom, m2b), axis=0, keepdims=True)
     misc = jnp.where(sub8 == 0, as_row(w2b), jnp.where(sub8 == 1, as_row(m2b), jnp.broadcast_to(share, (8, LANE))))
 
-    fin[1, q, zpos, rpos, 0:size_a, :] = mom[span[0], :]
-    fin[1, q, zpos, rpos, size_a:urows, :] = mom[own_share(), :]
-    fin[1, q, zpos, rpos, urows:urows + 8, :] = misc
+    stage(1, mom, misc)
     spread(1)
     over(0)
     relay(1)
@@ -497,7 +501,7 @@
             fin_pair(arr, w).wait()
         for d in order:
             fin_ring(arr, d).wait_send()
-            for e in range(side):
+            for e in range(side + 1):
                 fin_cross(arr, e, d).wait_send()
 
 
@@ -505,8 +509,8 @@
     side, hidden, feat, rows, hs, step, sizes = cfg
     chains = fin.shape[1]
     tiles = Tiles(side, feat, hs)
-    base = (0, tiles.size[0])
-    urows = tiles.size[0] + tiles.size[1]
+    base = (0, tiles.size[0] + 8)
+    extra = tiles.size[0]
     f32 = jnp.float32
     width = -(-hidden // LANE) * LANE
     lane = lax.broadcasted_iota(jnp.int32, (8, width), 1)
@@ -514,13 +518,13 @@
         acc = jnp.zeros((8, width), f32)
         tot = jnp.zeros((8, LANE), f32)
         for z in range(side):
-            tile = fin[1, ch, z, 0, urows:urows + 8, :]
+            tile = fin[1, ch, z, 0, extra:extra + 8, :]
             wide = jnp.concatenate([tile, jnp.zeros((8, width - LANE), f32)], axis=1)
             r0 = min(z * hs, hidden - hs)
             wide = pltpu.roll(wide, r0, 1) if r0 else wide
             acc = jnp.where((lane >= z * hs) & (lane < (z + 1) * hs), wide, acc)
             for r in range(side):
-                tot = tot + fin[1, ch, z, r, urows:urows + 8, :]
+                tot = tot + fin[1, ch, z, r, extra:extra + 8, :]
         w_row[ch:ch + 1, :] = acc[0:1, 0:hidden]
         m_row[ch:ch + 1, :] = acc[1:2, 0:hidden]
         energy[ch] = jnp.sum(tot[2:3, :])
@@ -616,7 +620,7 @@
                     dma((2 + pieces,)), dma((7, pieces)), dma((7, pieces)), dma((8,)), dma((9,)),
                     dma((2, groups, side)), dma((2, groups, side)),
                     dma((3, side)), dma((3, side)), dma((side,)), dma((side,)),
-                    dma((2, side)), dma((2, side)), dma((2, side, side)), dma((2, side, side)),
+                    dma((2, side)), dma((2, side)), dma((2, side + 1, side)), dma((2, side + 1, side)),
                     dma((2, side)), dma((2, side)),
                 ],
                 compiler_params=pltpu.CompilerParams(collective_id=0, has_side_effects=True, vmem_limit_bytes=67043328 - 4 * math.prod(piece_shape)),

time: 312 us -> 308 us (0.987)
  Pallas kernels: 311 us -> 307 us
    pallas_call x1, Pallas kernels: 308 us -> 305 us  [device_body(): pl.pallas_call(functools.partial(_kernel, cfg), out_shape=vm(piece_shape,...]
where the time goes in v5:
time: 308 us
  Pallas kernels  307 us (100%)
    pallas_call x1, Pallas kernels, device_body(): pl.pallas_call(functools.partial(_kernel, cfg), out_shape=vm(piece_shape,...  305 us

profile of v5, /device:TPU:97, one launch (start us, length us, event | category | flops | bytes accessed | tf_op | source)
XLA Modules:
  0.0 308.2 jit_solution(14950494687631438484)
XLA Ops:
  0.6 304.7 %shard_map.101.fin = f32[2,2,4,4,168,128]{5,4,3,2,1,0:T(8,128)S(1)} custom-call(bf16[784,1024]{1,0:T(8,128)(2,1)} %bitcast.8, s32[8,128]{1,0:T(8,128)} %bitcast.9, f32[2,400,784]{2,1,0:T(8,128)} %bitcast.6, f32[2,400,784]{2,1,0:T(8,128)} %bitcast.7, f32[2,400]{1,0:T(2,128)} %wo_hbm.1, f32[2,400]{1,0:T(2,128)} %mo_hbm.1), custom_call_target="tpu_custom_call" | custom-call | tf_op jit(solution)/shard_map/pallas_call | solution.py:590
  305.3 2.7 shard_map.102
